TPU v7x, 128 devices: a whole 4x4x4 slice. The times are simulated.
128 devices in a mesh: row: 16 (over x, y), col: 8 (over z, core).
Axes of the slice: x: 4, y: 4, z: 4, core: 2. Of those that a mesh axis runs over, the one named last changes fastest.
Arguments:
- weights: int32 [8192, 8192], P('row', 'col'), may hold values from 1 to 64
Outputs:
- distances: int32 [8192, 8192], P('row', 'col')
All inputs are finite; a program needn't handle non-finite values.
Results may differ from a plain program's by a relative error of at most 0.000001.
Values may be sent and summed in bfloat16 or wider, within the bound.
No kernel may reach another device: no remote copies, remote signals or barrier semaphores. Data moves between devices by JAX's collectives and lax.ppermute only.
A program may use at most 64 MiB of HBM per device.

v0:
```python
import jax
import jax.numpy as jnp
from jax import lax
from jax.sharding import PartitionSpec as P

PIVOT = 128
STEPS = 4


def broadcast(array, axis, root):
    return lax.dynamic_index_in_dim(lax.all_gather(array, axis), root, 0, keepdims=False)


def min_plus(acc, left, right):
    group = 8
    count = left.shape[1] // group

    def update(index, total):
        begin = (index * group).astype(jnp.int32)
        left_part = lax.dynamic_slice_in_dim(left, begin, group, 1)
        right_part = lax.dynamic_slice_in_dim(right, begin, group, 0)
        return jnp.minimum(total, jnp.min(left_part[:, :, None] + right_part[None, :, :], axis=1))

    return lax.fori_loop(0, count, update, acc)


def close_block(block):

    def relax(vertex, current):
        vertex = jnp.asarray(vertex).astype(jnp.int32)
        column = lax.dynamic_slice_in_dim(current, vertex, 1, 1)
        across = lax.dynamic_slice_in_dim(current, vertex, 1, 0)
        return jnp.minimum(current, column + across)

    return lax.fori_loop(0, block.shape[0], relax, block)


def per_device(weights):
    rows_dev, cols_dev = weights.shape
    verts = rows_dev * lax.axis_size("row")
    stride = verts // STEPS
    row_ids = lax.axis_index("row") * rows_dev + jnp.arange(rows_dev, dtype=jnp.int32)
    col_ids = lax.axis_index("col") * cols_dev + jnp.arange(cols_dev, dtype=jnp.int32)
    dist = jnp.where(row_ids[:, None] == col_ids[None, :], jnp.int32(0), weights).astype(jnp.int32)
    for step in range(STEPS):
        first = step * stride
        row_root = first // rows_dev
        row_off = first - row_root * rows_dev
        col_root = first // cols_dev
        col_off = first - col_root * cols_dev
        strip_rows = dist[row_off : row_off + PIVOT, :]
        strip_cols = dist[:, col_off : col_off + PIVOT]
        panel_rows = jax.tree.map(lambda part: broadcast(part, "row", row_root), strip_rows)
        closed = close_block(panel_rows[:, col_off : col_off + PIVOT])
        new_cols = min_plus(strip_cols, strip_cols, closed)
        panel_cols = jax.tree.map(lambda part: broadcast(part, "col", col_root), new_cols)
        dist = min_plus(dist, panel_cols, panel_rows)
    return dist


def solution(mesh):
    placed = (P("row", "col"),)
    return jax.shard_map(
        per_device, mesh=mesh, in_specs=placed, out_specs=P("row", "col"), check_vma=False
    )
```

profile of v0, /device:TPU:1, one launch (start us, length us, event | category | flops | bytes accessed | tf_op | source)
XLA Modules:
  0.0 1272.3 jit_solution(7129442671943326020)
XLA Ops:
  9.3 73.7 %all-gather.17.cloned.1.call-done = s32[2048,1024]{1,0:T(8,128)} async-done(((s32[128,1024]{1,0:T(8,128)}), s32[2048,1024]{1,0:T(8,128)}) %all-gather.17.cloned.1.call-update) | async-done | bytes 8388624 | tf_op jit(solution)/shard_map/all_gather | solution.py:11
  83.8 38.9 %while.156 = (s32[]{:T(128)}, s32[128,128]{1,0:T(8,128)S(1)}, s32[]{:T(128)}) while((s32[]{:T(128)}, s32[128,128]{1,0:T(8,128)S(1)}, s32[]{:T(128)}) %tuple.281), condition=%wide.region_1.2_spmd, body=%wide.region_0.1_spmd.sunk | while | flops 32770 | bytes 134205 | solution.py:35
  122.7 50.6 %while.157 = (s32[]{:T(128)}, s32[512,128]{1,0:T(8,128)S(1)}, s32[512,128]{1,0:T(8,128)S(1)}, s32[128,128]{1,0:T(8,128)S(1)}, s32[]{:T(128)}, /*index=5*/s32[]{:T(128)}, s32[]{:T(128)}, s32[]{:T(128)}) while((s32[]{:T(128)}, s32[512,128]{1,0:T(8,128)S(1)}, s32[512,128]{1,0:T(8,128)S(1)}, s32[128,128]{1,0:T(8,128)S(1)}, s32[]{:T(128)}, ...), condition=%wide.region_4.5_spmd, body=%wide.region_2.4_spmd.sunk | while | flops 1048582 | bytes 1110155 | solution.py:24
  174.1 26.0 %all-gather.19.cloned.1.call-done = s32[4096,128]{1,0:T(8,128)} async-done(((s32[512,128]{1,0:T(8,128)}), s32[4096,128]{1,0:T(8,128)}) %all-gather.19.cloned.1.call-update) | async-done | bytes 2097168 | tf_op jit(solution)/shard_map/all_gather | solution.py:11
  201.1 123.8 %while.158 = (s32[]{:T(128)}, s32[512,1024]{1,0:T(8,128)S(1)}, s32[512,128]{1,0:T(8,128)S(1)}, s32[128,1024]{1,0:T(8,128)S(1)}, s32[]{:T(128)}, /*index=5*/s32[]{:T(128)}, s32[]{:T(128)}, s32[]{:T(128)}) while((s32[]{:T(128)}, s32[512,1024]{1,0:T(8,128)S(1)}, s32[512,128]{1,0:T(8,128)S(1)}, s32[128,1024]{1,0:T(8,128)S(1)}, s32[]{:T(128)}, ...), condition=%wide.region_7.8_spmd, body=%wide.region_5.7_spmd.sunk | while | flops 8388614 | bytes 8536203 | solution.py:24
  201.3 6.9 add_reduce_fusion.17
  209.0 6.9 add_reduce_fusion.17
  216.8 6.9 add_reduce_fusion.17
  224.5 6.9 add_reduce_fusion.17
  232.2 6.9 add_reduce_fusion.17
  240.0 6.9 add_reduce_fusion.17
  247.7 6.9 add_reduce_fusion.17
  255.4 6.9 add_reduce_fusion.17
  301.9 6.9 add_reduce_fusion.17
  309.6 6.9 add_reduce_fusion.17
  317.3 6.9 add_reduce_fusion.17
  325.9 70.1 %all-gather.21.cloned.1.call-done = s32[2048,1024]{1,0:T(8,128)} async-done(((s32[128,1024]{1,0:T(8,128)}), s32[2048,1024]{1,0:T(8,128)}) %all-gather.21.cloned.1.call-update) | async-done | bytes 8388624 | tf_op jit(solution)/shard_map/all_gather | solution.py:11
  396.9 38.9 %while.159 = (s32[]{:T(128)}, s32[128,128]{1,0:T(8,128)S(1)}, s32[]{:T(128)}) while((s32[]{:T(128)}, s32[128,128]{1,0:T(8,128)S(1)}, s32[]{:T(128)}) %tuple.290), condition=%wide.region_9.10_spmd, body=%wide.region_8.9_spmd.sunk | while | flops 32770 | bytes 134205 | solution.py:35
  435.8 50.6 %while.160 = (s32[]{:T(128)}, s32[512,128]{1,0:T(8,128)S(1)}, s32[512,128]{1,0:T(8,128)S(1)}, s32[128,128]{1,0:T(8,128)S(1)}, s32[]{:T(128)}, /*index=5*/s32[]{:T(128)}, s32[]{:T(128)}, s32[]{:T(128)}) while((s32[]{:T(128)}, s32[512,128]{1,0:T(8,128)S(1)}, s32[512,128]{1,0:T(8,128)S(1)}, s32[128,128]{1,0:T(8,128)S(1)}, s32[]{:T(128)}, ...), condition=%wide.region_12.13_spmd, body=%wide.region_10.12_spmd.sunk | while | flops 1048582 | bytes 1110155 | solution.py:24
  487.2 26.0 %all-gather.23.cloned.1.call-done = s32[4096,128]{1,0:T(8,128)} async-done(((s32[512,128]{1,0:T(8,128)}), s32[4096,128]{1,0:T(8,128)}) %all-gather.23.cloned.1.call-update) | async-done | bytes 2097168 | tf_op jit(solution)/shard_map/all_gather | solution.py:11
  514.2 123.8 %while.161 = (s32[]{:T(128)}, s32[512,1024]{1,0:T(8,128)S(1)}, s32[512,128]{1,0:T(8,128)S(1)}, s32[128,1024]{1,0:T(8,128)S(1)}, s32[]{:T(128)}, /*index=5*/s32[]{:T(128)}, s32[]{:T(128)}, s32[]{:T(128)}) while((s32[]{:T(128)}, s32[512,1024]{1,0:T(8,128)S(1)}, s32[512,128]{1,0:T(8,128)S(1)}, s32[128,1024]{1,0:T(8,128)S(1)}, s32[]{:T(128)}, ...), condition=%wide.region_15.16_spmd, body=%wide.region_13.15_spmd.sunk | while | flops 8388614 | bytes 8536203 | solution.py:24
  529.8 6.9 add_reduce_fusion.19
  553.0 6.9 add_reduce_fusion.19
  576.3 6.9 add_reduce_fusion.19
  584.0 6.9 add_reduce_fusion.19
  607.2 6.9 add_reduce_fusion.19
  630.4 6.9 add_reduce_fusion.19
  639.0 70.1 %all-gather.25.cloned.1.call-done = s32[2048,1024]{1,0:T(8,128)} async-done(((s32[128,1024]{1,0:T(8,128)}), s32[2048,1024]{1,0:T(8,128)}) %all-gather.25.cloned.1.call-update) | async-done | bytes 8388624 | tf_op jit(solution)/shard_map/all_gather | solution.py:11
  710.0 38.9 %while.162 = (s32[]{:T(128)}, s32[128,128]{1,0:T(8,128)S(1)}, s32[]{:T(128)}) while((s32[]{:T(128)}, s32[128,128]{1,0:T(8,128)S(1)}, s32[]{:T(128)}) %tuple.299), condition=%wide.region_17.18_spmd, body=%wide.region_16.17_spmd.sunk | while | flops 32770 | bytes 134205 | solution.py:35
  748.9 50.6 %while.163 = (s32[]{:T(128)}, s32[512,128]{1,0:T(8,128)S(1)}, s32[512,128]{1,0:T(8,128)S(1)}, s32[128,128]{1,0:T(8,128)S(1)}, s32[]{:T(128)}, /*index=5*/s32[]{:T(128)}, s32[]{:T(128)}, s32[]{:T(128)}) while((s32[]{:T(128)}, s32[512,128]{1,0:T(8,128)S(1)}, s32[512,128]{1,0:T(8,128)S(1)}, s32[128,128]{1,0:T(8,128)S(1)}, s32[]{:T(128)}, ...), condition=%wide.region_20.21_spmd, body=%wide.region_18.20_spmd.sunk | while | flops 1048582 | bytes 1110155 | solution.py:24
  800.5 25.8 %all-gather.27.cloned.1.call-done = s32[4096,128]{1,0:T(8,128)} async-done(((s32[512,128]{1,0:T(8,128)}), s32[4096,128]{1,0:T(8,128)}) %all-gather.27.cloned.1.call-update) | async-done | bytes 2097168 | tf_op jit(solution)/shard_map/all_gather | solution.py:11
  827.3 123.8 %while.164 = (s32[]{:T(128)}, s32[512,1024]{1,0:T(8,128)S(1)}, s32[512,128]{1,0:T(8,128)S(1)}, s32[128,1024]{1,0:T(8,128)S(1)}, s32[]{:T(128)}, /*index=5*/s32[]{:T(128)}, s32[]{:T(128)}, s32[]{:T(128)}) while((s32[]{:T(128)}, s32[512,1024]{1,0:T(8,128)S(1)}, s32[512,128]{1,0:T(8,128)S(1)}, s32[128,1024]{1,0:T(8,128)S(1)}, s32[]{:T(128)}, ...), condition=%wide.region_23.24_spmd, body=%wide.region_21.23_spmd.sunk | while | flops 8388614 | bytes 8536203 | solution.py:24
  842.9 6.9 add_reduce_fusion.21
  866.1 6.9 add_reduce_fusion.21
  889.4 6.9 add_reduce_fusion.21
  912.6 6.9 add_reduce_fusion.21
  935.8 6.9 add_reduce_fusion.21
  952.1 70.1 %all-gather.29.cloned.1.call-done = s32[2048,1024]{1,0:T(8,128)} async-done(((s32[128,1024]{1,0:T(8,128)}), s32[2048,1024]{1,0:T(8,128)}) %all-gather.29.cloned.1.call-update) | async-done | bytes 8388624 | tf_op jit(solution)/shard_map/all_gather | solution.py:11
  1023.1 38.9 %while.165 = (s32[]{:T(128)}, s32[128,128]{1,0:T(8,128)S(1)}, s32[]{:T(128)}) while((s32[]{:T(128)}, s32[128,128]{1,0:T(8,128)S(1)}, s32[]{:T(128)}) %tuple.308), condition=%wide.region_25.26_spmd, body=%wide.region_24.25_spmd.sunk | while | flops 32770 | bytes 134205 | solution.py:35
  1062.0 50.6 %while.166 = (s32[]{:T(128)}, s32[512,128]{1,0:T(8,128)S(1)}, s32[512,128]{1,0:T(8,128)S(1)}, s32[128,128]{1,0:T(8,128)S(1)}, s32[]{:T(128)}, /*index=5*/s32[]{:T(128)}, s32[]{:T(128)}, s32[]{:T(128)}) while((s32[]{:T(128)}, s32[512,128]{1,0:T(8,128)S(1)}, s32[512,128]{1,0:T(8,128)S(1)}, s32[128,128]{1,0:T(8,128)S(1)}, s32[]{:T(128)}, ...), condition=%wide.region_28.29_spmd, body=%wide.region_26.28_spmd.sunk | while | flops 1048582 | bytes 1110155 | solution.py:24
  1113.3 26.1 %all-gather.31.cloned.1.call-done = s32[4096,128]{1,0:T(8,128)} async-done(((s32[512,128]{1,0:T(8,128)}), s32[4096,128]{1,0:T(8,128)}) %all-gather.31.cloned.1.call-update) | async-done | bytes 2097168 | tf_op jit(solution)/shard_map/all_gather | solution.py:11
  1140.4 123.8 %while.167 = (s32[]{:T(128)}, s32[512,1024]{1,0:T(8,128)S(1)}, s32[512,128]{1,0:T(8,128)S(1)}, s32[128,1024]{1,0:T(8,128)S(1)}, s32[]{:T(128)}, /*index=5*/s32[]{:T(128)}, s32[]{:T(128)}, s32[]{:T(128)}) while((s32[]{:T(128)}, s32[512,1024]{1,0:T(8,128)S(1)}, s32[512,128]{1,0:T(8,128)S(1)}, s32[128,1024]{1,0:T(8,128)S(1)}, s32[]{:T(128)}, ...), condition=%wide.region_31.32_spmd, body=%wide.region_29.31_spmd.sunk | while | flops 8388614 | bytes 8536203 | solution.py:24
  1140.5 6.9 add_reduce_fusion.23
  1156.0 6.9 add_reduce_fusion.23
  1194.7 6.9 add_reduce_fusion.23
  1210.2 6.9 add_reduce_fusion.23
  1233.4 6.9 add_reduce_fusion.23
  1248.9 6.9 add_reduce_fusion.23
  (2077 shorter events, 652.8 us)
Async XLA Ops:
  6.5 76.5 %all-gather.17.cloned.1.call-start = ((), (), s32[]{:S(2)}) async-start(), calls=%async_computation | async-start | bytes 8912896 | tf_op jit(solution)/shard_map/all_gather | solution.py:11
  9.2 190.9 %all-gather.19.cloned.1.call-start = ((), (), s32[]{:S(2)}) async-start(), calls=%async_computation.1 | async-start | bytes 2359296 | tf_op jit(solution)/shard_map/all_gather | solution.py:11
  122.7 78.4 %slice-start.1 = ((s32[2048,1024]{1,0:T(8,128)}), s32[128,1024]{1,0:T(8,128)S(1)}, s32[]{:S(2)}) async-start(s32[2048,1024]{1,0:T(8,128)} %all-gather.17.cloned.1.call-done), calls=%async_computation.9 | async-start | bytes 1048576 | tf_op jit(solution)/shard_map/jit(dynamic_index_in_dim)/dynamic_slice | solution.py:11
  173.4 0.7 copy-start.1
  174.1 222.0 %all-gather.21.cloned.1.call-start = ((), (), s32[]{:S(2)}) async-start(), calls=%async_computation.2 | async-start | bytes 8912896 | tf_op jit(solution)/shard_map/all_gather | solution.py:11
  325.8 187.4 %all-gather.23.cloned.1.call-start = ((), (), s32[]{:S(2)}) async-start(), calls=%async_computation.3 | async-start | bytes 2359296 | tf_op jit(solution)/shard_map/all_gather | solution.py:11
  435.8 78.4 %slice-start.2 = ((s32[2048,1024]{1,0:T(8,128)}), s32[128,1024]{1,0:T(8,128)S(1)}, s32[]{:S(2)}) async-start(s32[2048,1024]{1,0:T(8,128)} %all-gather.21.cloned.1.call-done), calls=%async_computation.10 | async-start | bytes 1048576 | tf_op jit(solution)/shard_map/jit(dynamic_index_in_dim)/dynamic_slice | solution.py:11
  486.4 0.7 copy-start.2
  487.1 222.0 %all-gather.25.cloned.1.call-start = ((), (), s32[]{:S(2)}) async-start(), calls=%async_computation.4 | async-start | bytes 8912896 | tf_op jit(solution)/shard_map/all_gather | solution.py:11
  638.9 187.4 %all-gather.27.cloned.1.call-start = ((), (), s32[]{:S(2)}) async-start(), calls=%async_computation.5 | async-start | bytes 2359296 | tf_op jit(solution)/shard_map/all_gather | solution.py:11
  748.8 78.4 %slice-start.3 = ((s32[2048,1024]{1,0:T(8,128)}), s32[128,1024]{1,0:T(8,128)S(1)}, s32[]{:S(2)}) async-start(s32[2048,1024]{1,0:T(8,128)} %all-gather.25.cloned.1.call-done), calls=%async_computation.11 | async-start | bytes 1048576 | tf_op jit(solution)/shard_map/jit(dynamic_index_in_dim)/dynamic_slice | solution.py:11
  799.5 0.7 copy-start.3
  800.2 222.0 %all-gather.29.cloned.1.call-start = ((), (), s32[]{:S(2)}) async-start(), calls=%async_computation.6 | async-start | bytes 8912896 | tf_op jit(solution)/shard_map/all_gather | solution.py:11
  952.0 187.4 %all-gather.31.cloned.1.call-start = ((), (), s32[]{:S(2)}) async-start(), calls=%async_computation.7 | async-start | bytes 2359296 | tf_op jit(solution)/shard_map/all_gather | solution.py:11
  1061.9 78.4 %slice-start = ((s32[2048,1024]{1,0:T(8,128)}), s32[128,1024]{1,0:T(8,128)S(1)}, s32[]{:S(2)}) async-start(s32[2048,1024]{1,0:T(8,128)} %all-gather.29.cloned.1.call-done), calls=%async_computation.8 | async-start | bytes 1048576 | tf_op jit(solution)/shard_map/jit(dynamic_index_in_dim)/dynamic_slice | solution.py:11
  1112.6 0.7 copy-start.4
  1264.2 1.3 copy-start
Sparse Core Ops, SparseCore 0:
  9.5 73.4 all-gather.16
  174.2 25.8 all-gather.18
  325.9 70.0 all-gather.20
  487.3 25.8 all-gather.22
  639.0 70.0 all-gather.24
  800.4 25.8 all-gather.26
  952.1 70.0 all-gather.28
  1113.4 25.8 all-gather.30
where the time goes:
time: 1270 us
  other arithmetic  719 us (57%)
  waiting for transfers between devices  388 us (31%)
  local copies, waits for them, and re-layouts  127 us (10%)
  loops' own time  24.3 us (2%)
  between operations  13.8 us (1%)
    reduce_min x128, other arithmetic, update(): jnp.min(left_part[:, :, None] + right_part[None, :, :], axis=1)  628 us
    all_gather x8, waiting for transfers between devices, broadcast(): lax.all_gather(array, axis)  388 us
    dynamic_slice x512, local copies, waits for them, and re-layouts, relax(): column = lax.dynamic_slice_in_dim(current, vertex, 1, 1)  88.4 us
    min x128, other arithmetic, update(): jnp.minimum(total, jnp.min(left_part[:, :, None] + right_part[None, :, :]...  45.4 us
    min x512, other arithmetic, relax(): return jnp.minimum(current, column + across)  43.1 us
  transfers between devices with their start and end apart: 8, of which 8 were waited for; matrix products, arithmetic and copies ran while one was open for 0% of the time, Pallas kernels for 0%

commit v1 on v0

v1 whole, which is shorter than its diff:
```python
import jax
import jax.numpy as jnp
from jax import lax
from jax.experimental import pallas as pl
from jax.experimental.pallas import tpu as pltpu
from jax.sharding import PartitionSpec as P

PIVOT = 128
STEPS = 4
SIDE = 4
HALF = 2 * PIVOT
SIZE = STEPS * PIVOT
PART = PIVOT // SIDE
F32, BF16 = jnp.float32, jnp.bfloat16
RATE = 8.0625
LN2 = 0.6931471805599453
SLACK = 0.004
LEFT, RIGHT = 6, 7
SQUARINGS = 6
LINE = [[SIDE * i + k for k in range(SIDE)] for i in range(SIDE)]
COLUMN = [[SIDE * k + i for k in range(SIDE)] for i in range(SIDE)]
COL_LINE = [[2 * k + c for k in range(SIDE)] for c in range(2)]
PAIR = [[2 * k, 2 * k + 1] for k in range(SIDE)]


def encode(value):
    far = value >= BF16(33.0)
    a = value - jnp.where(far, BF16(33.0), BF16(1.0))
    scale = jnp.exp2(BF16(125.0) - BF16(8.0) * a) * jnp.exp2(BF16(-0.0625) * a)
    zero = jnp.zeros_like(scale)
    lo = jnp.where(far, zero, scale)
    t5 = jnp.where(far, scale * BF16(2.0**-11), zero)
    mid = jnp.where(value >= BF16(17.0), lo, zero)
    t1 = lo * BF16(2.0**-66)
    t4 = t1 * BF16(2.0**-62)
    t3 = t5 * BF16(2.0**-119)
    return t1, lo, t3, t4, t5, mid


def left_tables(tables):
    t1, t2, t3, t4, t5, mid = tables
    return t1, t4, t3, t2, t5, mid * BF16(2.0**124)


def right_tables(tables):
    t1, t2, t3, t4, t5, mid = tables
    return t1, t3, t4, t2, t5, t2, mid * BF16(2.0**123)


def decode(s1, s2, s3):
    near = s1 >= 2.0**-59.4
    middle = s2 >= 2.0**-121
    s = jnp.where(near, s1, jnp.where(middle, s2, s3))
    p1, p2, p3 = (p / RATE - SLACK + 2.0 for p in (118.0, 250.0, 497.0))
    p = jnp.where(near, p1, jnp.where(middle, p2, p3))
    return jnp.ceil(p - jnp.log(s) * (1.0 / (RATE * LN2)))


def dot(left, right):
    return jnp.dot(left, right, preferred_element_type=F32)


def put_left(left_ref, at, tables):
    for t, table in enumerate(left_tables(tables)):
        left_ref[at, t * HALF : (t + 1) * HALF] = table


def put_right(right_ref, at, size, tables):
    for t, table in enumerate(right_tables(tables)):
        right_ref[pl.ds(t * HALF + at, size), :] = table


def sums(left_ref, right_ref, rows, cols):
    return (
        dot(left_ref[rows, :HALF], right_ref[:HALF, cols]),
        dot(left_ref[rows, HALF : 4 * HALF], right_ref[HALF : 4 * HALF, cols]),
        dot(left_ref[rows, 3 * HALF : 6 * HALF], right_ref[4 * HALF : 7 * HALF, cols]),
    )


CHUNK = 32


def lower(ref, rows, cols, windows):
    for i in range(0, windows[0].shape[0], CHUNK):
        at = slice(rows + i, rows + i + CHUNK)
        new = decode(*(w[i : i + CHUNK] for w in windows))
        ref[at, cols] = jnp.minimum(ref[at, cols].astype(F32), new).astype(BF16)


def encode_rows(ref, rows, cols, count, left=None, right=None):
    for i in range(0, count, CHUNK):
        tables = encode(ref[rows + i : rows + i + CHUNK, cols])
        if left is not None:
            put_left(left, slice(i, i + CHUNK), tables)
        if right is not None:
            put_right(right, i, CHUNK, tables)


def close(x_ref, at, left_ref, right_ref):
    cols = slice(at, at + HALF)

    def square(_, carry):
        encode_rows(x_ref, at, cols, HALF, left_ref, right_ref)
        lower(x_ref, at, cols, sums(left_ref, right_ref, slice(0, HALF), slice(0, HALF)))
        return carry

    lax.fori_loop(0, SQUARINGS, square, 0)


def multiply(ref, cols, source, source_cols, left_ref, right_ref, first, count):
    for r in range(first, first + count, HALF):
        encode_rows(source, r, source_cols, HALF, left=left_ref)
        lower(ref, r, cols, sums(left_ref, right_ref, slice(0, HALF), slice(0, HALF)))


P_, Q_ = slice(0, HALF), slice(HALF, SIZE)


def closure_kernel(index_ref, *refs):
    blocks = refs[:SIDE]
    x_ref, left_ref, right_ref = refs[SIDE:]
    for shift in range(SIDE):
        col = pl.multiple_of(lax.rem(index_ref[2] + SIDE - shift, SIDE) * PIVOT, PIVOT)
        for other in range(SIDE):
            row = pl.multiple_of(lax.rem(index_ref[0] + SIDE - other, SIDE) * PIVOT, PIVOT)
            x_ref[pl.ds(row, PIVOT), pl.ds(col, PIVOT)] = blocks[shift][other]
    close(x_ref, 0, left_ref, right_ref)
    encode_rows(x_ref, 0, P_, HALF, right=right_ref)
    multiply(x_ref, P_, x_ref, P_, left_ref, right_ref, HALF, HALF)
    encode_rows(x_ref, 0, Q_, HALF, right=right_ref)
    multiply(x_ref, Q_, x_ref, P_, left_ref, right_ref, HALF, HALF)
    close(x_ref, HALF, left_ref, right_ref)


def chain_kernel(index_ref, x_ref, *refs):
    panels = refs[:SIDE]
    own_ref, left_ref, right_ref = refs[SIDE:]
    rows = own_ref.shape[0]
    for shift in range(SIDE):
        col = pl.multiple_of(lax.rem(index_ref[2] + SIDE - shift, SIDE) * PIVOT, PIVOT)
        own_ref[:, pl.ds(col, PIVOT)] = panels[shift][...]
    for at, cols, to, source in ((0, P_, P_, P_), (0, Q_, Q_, P_), (HALF, Q_, Q_, Q_), (HALF, P_, P_, Q_)):
        encode_rows(x_ref, at, cols, HALF, right=right_ref)
        multiply(own_ref, to, own_ref, source, left_ref, right_ref, 0, rows)


def final_kernel(index_ref, own_ref, *refs):
    pieces = refs[:SIDE]
    weights_ref, out_ref, left_ref, right_ref = refs[SIDE:]
    rows, width = weights_ref.shape
    tile = pl.program_id(0)

    @pl.when(tile == 0)
    def _():
        for chunk in range(2):
            encode_rows(own_ref, 0, slice(chunk * HALF, (chunk + 1) * HALF), rows, left=left_ref.at[chunk])

    for shift in range(SIDE):
        for other in range(SIDE):
            s = lax.rem(index_ref[0] + SIDE - other, SIDE)
            q = lax.rem(index_ref[1] + SIDE - shift, SIDE)
            base = (s // 2) * (RIGHT * HALF) + lax.rem(s, 2) * PIVOT + q * PART
            for t, table in enumerate(right_tables(encode(pieces[shift][other]))):
                right_ref[pl.ds(pl.multiple_of(base + t * HALF, PART), PART), :] = table
    diagonal = index_ref[3] - tile * width
    for r in range(0, rows, HALF):
        parts = [
            sums(
                left_ref.at[chunk],
                right_ref.at[chunk * RIGHT * HALF : (chunk + 1) * RIGHT * HALF],
                slice(r, r + HALF),
                slice(0, width),
            )
            for chunk in range(2)
        ]
        for i in range(0, HALF, CHUNK):
            row = slice(r + i, r + i + CHUNK)
            new = decode(*(jnp.maximum(a[i : i + CHUNK], b[i : i + CHUNK]) for a, b in zip(*parts)))
            best = jnp.minimum(weights_ref[row, :].astype(F32), new).astype(jnp.int32)
            down = lax.broadcasted_iota(jnp.int32, best.shape, 0)
            across = lax.broadcasted_iota(jnp.int32, best.shape, 1)
            out_ref[row, :] = jnp.where(across - down == diagonal + (r + i), 0, best)


SMEM = pl.BlockSpec(memory_space=pltpu.SMEM)
VMEM = pl.BlockSpec(memory_space=pltpu.VMEM)


def cost(flops):
    return pl.CostEstimate(flops=flops, bytes_accessed=2_000_000, transcendentals=0)


def closure_call(index, blocks):
    return pl.pallas_call(
        closure_kernel,
        out_shape=jax.ShapeDtypeStruct((SIZE, SIZE), BF16),
        in_specs=[SMEM] + [VMEM] * SIDE,
        out_specs=VMEM,
        scratch_shapes=[pltpu.VMEM((HALF, LEFT * HALF), BF16), pltpu.VMEM((RIGHT * HALF, HALF), BF16)],
        cost_estimate=cost(10_000_000_000),
        name="closure",
    )(index, *blocks)


def chain_call(index, x, panels):
    rows = panels[0].shape[0]
    return pl.pallas_call(
        chain_kernel,
        out_shape=jax.ShapeDtypeStruct((rows, SIZE), BF16),
        in_specs=[SMEM, VMEM] + [VMEM] * SIDE,
        out_specs=VMEM,
        scratch_shapes=[pltpu.VMEM((HALF, LEFT * HALF), BF16), pltpu.VMEM((RIGHT * HALF, HALF), BF16)],
        cost_estimate=cost(4_000_000_000),
        name="chain",
    )(index, x, *panels)


def final_call(index, own, pieces, weights, width=256):
    rows, cols = weights.shape
    return pl.pallas_call(
        final_kernel,
        grid=(cols // width,),
        out_shape=jax.ShapeDtypeStruct((rows, cols), jnp.int32),
        in_specs=[SMEM, pl.BlockSpec((rows, SIZE), lambda j: (0, 0))]
        + [pl.BlockSpec((SIDE, PART, width), lambda j: (0, 0, j))] * SIDE
        + [pl.BlockSpec((rows, width), lambda j: (0, j))],
        out_specs=pl.BlockSpec((rows, width), lambda j: (0, j)),
        scratch_shapes=[
            pltpu.VMEM((2, rows, LEFT * HALF), BF16),
            pltpu.VMEM((2 * RIGHT * HALF, width), BF16),
        ],
        cost_estimate=cost(4_000_000_000),
        name="final",
    )(index, own, *pieces, weights)


def gather_line(array, axis, lines):
    got = {0: array}
    for shift in (1, 3, 2):
        pairs = [(line[i], line[(i + shift) % SIDE]) for line in lines for i in range(SIDE)]
        got[shift] = lax.ppermute(array, axis, pairs)
    return [got[shift] for shift in range(SIDE)]


def per_device(weights):
    rows, cols = weights.shape
    row, col = lax.axis_index("row"), lax.axis_index("col")
    index = jnp.stack([row // SIDE, row % SIDE, col // 2, row * rows - col * cols]).astype(jnp.int32)
    panel = weights[:, :PIVOT].astype(BF16)
    strip = weights[:PIVOT, :].astype(BF16)
    panel = lax.all_gather(panel, "col", axis_index_groups=PAIR)[0]
    block = panel[:PIVOT].reshape(SIDE * SIDE, cols)
    message = jnp.concatenate([strip[:PART], block])
    for y in range(1, SIDE):
        sent = jnp.concatenate([strip[y * PART : (y + 1) * PART], block])
        got = lax.ppermute(sent, "row", [(line[0], line[y]) for line in LINE])
        message = jnp.where(row % SIDE == y, got, message)
    panels = gather_line(panel, "col", COL_LINE)
    along_x = gather_line(message, "row", COLUMN)
    quarters = jnp.stack([m[:PART] for m in along_x])
    blocks = jnp.stack([m[PART:].reshape(PIVOT, PIVOT) for m in along_x])
    blocks = gather_line(blocks, "col", COL_LINE)
    pieces = gather_line(quarters, "row", LINE)
    x = closure_call(index, blocks)
    own = chain_call(index, x, panels)
    return final_call(index, own, pieces, weights)


def solution(mesh):
    placed = (P("row", "col"),)
    return jax.shard_map(
        per_device, mesh=mesh, in_specs=placed, out_specs=P("row", "col"), check_vma=False
    )
```

time: 1270 us -> 68.8 us (0.05)
  the two profiles are of different devices: /device:TPU:1 before, /device:TPU:0 now
where the time goes in v1:
time: 68.8 us; the launch traced here: 68.5 us
  starting transfers between devices  28.5 us (41%)
  Pallas kernels  23.4 us (34%)
  waiting for transfers between devices  8.75 us (13%)
  local copies, waits for them, and re-layouts  3.14 us (5%)
  other arithmetic  2.51 us (4%)
  blocking collectives  1.99 us (3%)
    ppermute x12, starting transfers between devices, gather_line(): got[shift] = lax.ppermute(array, axis, pairs)  21.4 us
    pallas_call x1, Pallas kernels, closure_call(): pl.pallas_call(closure_kernel, out_shape=jax.ShapeDtypeStruct((SIZE, SIZE...  9.33 us
    pallas_call x1, Pallas kernels, final_call(): pl.pallas_call(final_kernel, grid=(cols // width,), out_shape=jax.ShapeDt...  8.88 us
    ppermute x12, waiting for transfers between devices, gather_line(): got[shift] = lax.ppermute(array, axis, pairs)  7.16 us
    ppermute x3, starting transfers between devices, per_device(): got = lax.ppermute(sent, 'row', [(line[0], line[y]) for line in LINE])  7.07 us
    pallas_call x1, Pallas kernels, chain_call(): pl.pallas_call(chain_kernel, out_shape=jax.ShapeDtypeStruct((rows, SIZE),...  5.21 us
    unnamed x27, local copies, waits for them, and re-layouts  2.92 us
    all_gather x1, blocking collectives, per_device(): panel = lax.all_gather(panel, 'col', axis_index_groups=PAIR)[0]  1.99 us
  transfers between devices with their start and end apart: 15, of which 7 were waited for; matrix products, arithmetic and copies ran while one was open for 1% of the time, Pallas kernels for 21%

profile of v1, /device:TPU:0, one launch (start us, length us, event | category | flops | bytes accessed | tf_op | source)
XLA Modules:
  0.0 68.5 jit_solution(5473579527166585465)
XLA Ops:
  0.0 1.8 %convert.4 = bf16[512,1024]{1,0:T(8,128)(2,1)S(1)} convert(s32[512,1024]{1,0:T(8,128)} %refs_4_.1) | non-fusion elementwise | flops 524288 | bytes 3145728 | tf_op jit(solution)/shard_map/convert.1
  1.9 2.0 %all-gather = bf16[1024,128]{1,0:T(8,128)(2,1)S(1)} all-gather(bf16[512,128]{1,0:T(8,128)(2,1)S(1)} %slice.71), channel_id=2, replica_groups={{0,1},{2,3},{4,5},{6,7},{8,9},{10,11},{12,13},{14,15},{16,17},{18,19},{..., dimensions={0}, use_global_device_ids=true | all-gather | bytes 393216 | tf_op jit(solution)/shard_map/all_gather | solution.py:252
  3.9 0.0 copy-start.1
  3.9 4.2 %collective-permute-start.11 = (bf16[512,128]{1,0:T(8,128)(2,1)S(1)}, bf16[512,128]{1,0:T(8,128)(2,1)S(1)}, u32[]{:S(2)}, u32[]{:S(2)}) collective-permute-start(bf16[512,128]{1,0:T(8,128)(2,1)S(1)} %slice.80.refs_0_), channel_id=1, source_target_pairs={{0,6},{2,0},{4,2},{6,4},{1,7},{3,1},{5,3},{7,5},{8,14},{10,8},{12,... | collective-permute-start | bytes 393224 | tf_op jit(solution)/shard_map/ppermute | solution.py:242
  8.1 0.0 collective-permute-start.10
  8.2 3.5 %collective-permute-start.2 = (bf16[48,1024]{1,0:T(8,128)(2,1)S(1)}, bf16[48,1024]{1,0:T(8,128)(2,1)S(1)}, u32[]{:S(2)}, u32[]{:S(2)}) collective-permute-start(bf16[48,1024]{1,0:T(8,128)(2,1)S(1)} %get-tuple-element.9), channel_id=1, source_target_pairs={{0,8},{32,40},{64,72},{96,104},{1,9},{33,41},{65,73},{97,105},{2,1... | collective-permute-start | bytes 294920 | tf_op jit(solution)/shard_map/ppermute | solution.py:257
  11.7 2.3 %collective-permute-start.1 = (bf16[48,1024]{1,0:T(8,128)(2,1)S(1)}, bf16[48,1024]{1,0:T(8,128)(2,1)S(1)}, u32[]{:S(2)}, u32[]{:S(2)}) collective-permute-start(bf16[48,1024]{1,0:T(8,128)(2,1)S(1)} %get-tuple-element.10), channel_id=1, source_target_pairs={{0,16},{32,48},{64,80},{96,112},{1,17},{33,49},{65,81},{97,113},{2... | collective-permute-start | bytes 294920 | tf_op jit(solution)/shard_map/ppermute | solution.py:257
  14.0 1.3 %collective-permute-start = (bf16[48,1024]{1,0:T(8,128)(2,1)S(1)}, bf16[48,1024]{1,0:T(8,128)(2,1)S(1)}, u32[]{:S(2)}, u32[]{:S(2)}) collective-permute-start(bf16[48,1024]{1,0:T(8,128)(2,1)S(1)} %get-tuple-element.11), channel_id=1, source_target_pairs={{0,24},{32,56},{64,88},{96,120},{1,25},{33,57},{65,89},{97,121},{2... | collective-permute-start | bytes 294920 | tf_op jit(solution)/shard_map/ppermute | solution.py:257
  15.3 0.6 pad_add_fusion.index_ref
  15.9 0.0 collective-permute-done.2
  15.9 0.3 collective-permute-done.1
  16.2 1.3 %collective-permute-done = bf16[48,1024]{1,0:T(8,128)(2,1)S(1)} collective-permute-done((bf16[48,1024]{1,0:T(8,128)(2,1)S(1)}, bf16[48,1024]{1,0:T(8,128)(2,1)S(1)}, u32[]{:S(2)}, u32[]{:S(2)}) %collective-permute-start) | collective-permute-done | bytes 98336 | tf_op jit(solution)/shard_map/ppermute | solution.py:257
  17.5 0.1 fusion.2
  17.6 2.8 %collective-permute-start.5 = (bf16[48,1024]{1,0:T(8,128)(2,1)S(1)}, bf16[48,1024]{1,0:T(8,128)(2,1)S(1)}, u32[]{:S(2)}, u32[]{:S(2)}) collective-permute-start(bf16[48,1024]{1,0:T(8,128)(2,1)S(1)} %fusion.2), channel_id=1, source_target_pairs={{0,96},{32,0},{64,32},{96,64},{8,104},{40,8},{72,40},{104,72},{16,... | collective-permute-start | bytes 294920 | tf_op jit(solution)/shard_map/ppermute | solution.py:242
  20.4 0.8 %collective-permute-start.4 = (bf16[48,1024]{1,0:T(8,128)(2,1)S(1)}, bf16[48,1024]{1,0:T(8,128)(2,1)S(1)}, u32[]{:S(2)}, u32[]{:S(2)}) collective-permute-start(bf16[48,1024]{1,0:T(8,128)(2,1)S(1)} %fusion.2), channel_id=1, source_target_pairs={{0,64},{32,96},{64,0},{96,32},{8,72},{40,104},{72,8},{104,40},{16,... | collective-permute-start | bytes 294920 | tf_op jit(solution)/shard_map/ppermute | solution.py:242
  21.2 0.9 %collective-permute-start.3 = (bf16[48,1024]{1,0:T(8,128)(2,1)S(1)}, bf16[48,1024]{1,0:T(8,128)(2,1)S(1)}, u32[]{:S(2)}, u32[]{:S(2)}) collective-permute-start(bf16[48,1024]{1,0:T(8,128)(2,1)S(1)} %fusion.2), channel_id=1, source_target_pairs={{0,32},{32,64},{64,96},{96,0},{8,40},{40,72},{72,104},{104,8},{16,... | collective-permute-start | bytes 294920 | tf_op jit(solution)/shard_map/ppermute | solution.py:242
  22.1 2.0 %collective-permute-done.5 = bf16[48,1024]{1,0:T(8,128)(2,1)S(1)} collective-permute-done((bf16[48,1024]{1,0:T(8,128)(2,1)S(1)}, bf16[48,1024]{1,0:T(8,128)(2,1)S(1)}, u32[]{:S(2)}, u32[]{:S(2)}) %collective-permute-start.5) | collective-permute-done | bytes 98336 | tf_op jit(solution)/shard_map/ppermute | solution.py:242
  24.2 2.4 %collective-permute-done.4 = bf16[48,1024]{1,0:T(8,128)(2,1)S(1)} collective-permute-done((bf16[48,1024]{1,0:T(8,128)(2,1)S(1)}, bf16[48,1024]{1,0:T(8,128)(2,1)S(1)}, u32[]{:S(2)}, u32[]{:S(2)}) %collective-permute-start.4) | collective-permute-done | bytes 98336 | tf_op jit(solution)/shard_map/ppermute | solution.py:242
  26.6 1.0 %collective-permute-done.3 = bf16[48,1024]{1,0:T(8,128)(2,1)S(1)} collective-permute-done((bf16[48,1024]{1,0:T(8,128)(2,1)S(1)}, bf16[48,1024]{1,0:T(8,128)(2,1)S(1)}, u32[]{:S(2)}, u32[]{:S(2)}) %collective-permute-start.3) | collective-permute-done | bytes 98336 | tf_op jit(solution)/shard_map/ppermute | solution.py:242
  27.7 0.0 copy-start.2
  27.7 0.7 %collective-permute-start.8 = (bf16[4,128,128]{2,1,0:T(8,128)(2,1)S(1)}, bf16[4,128,128]{2,1,0:T(8,128)(2,1)S(1)}, u32[]{:S(2)}, u32[]{:S(2)}) collective-permute-start(bf16[4,128,128]{2,1,0:T(8,128)(2,1)S(1)} %constant_dynamic-update-slice_fusion.refs_0_), channel_id=1, source_target_pairs={{0,6},{2,0},{4,2},{6,4},{1,7},{3,1},{5,3},{7,5},{8,14},{10,8},{12,... | collective-permute-start | bytes 393224 | tf_op jit(solution)/shard_map/ppermute | solution.py:242
  28.4 3.0 %collective-permute-start.7 = (bf16[4,128,128]{2,1,0:T(8,128)(2,1)S(1)}, bf16[4,128,128]{2,1,0:T(8,128)(2,1)S(1)}, u32[]{:S(2)}, u32[]{:S(2)}) collective-permute-start(bf16[4,128,128]{2,1,0:T(8,128)(2,1)S(1)} %constant_dynamic-update-slice_fusion.refs_0_), channel_id=1, source_target_pairs={{0,4},{2,6},{4,0},{6,2},{1,5},{3,7},{5,1},{7,3},{8,12},{10,14},{12... | collective-permute-start | bytes 393224 | tf_op jit(solution)/shard_map/ppermute | solution.py:242
  31.4 1.3 %collective-permute-start.6 = (bf16[4,128,128]{2,1,0:T(8,128)(2,1)S(1)}, bf16[4,128,128]{2,1,0:T(8,128)(2,1)S(1)}, u32[]{:S(2)}, u32[]{:S(2)}) collective-permute-start(bf16[4,128,128]{2,1,0:T(8,128)(2,1)S(1)} %constant_dynamic-update-slice_fusion.refs_0_), channel_id=1, source_target_pairs={{0,2},{2,4},{4,6},{6,0},{1,3},{3,5},{5,7},{7,1},{8,10},{10,12},{12... | collective-permute-start | bytes 393224 | tf_op jit(solution)/shard_map/ppermute | solution.py:242
  32.8 0.0 copy-start
  32.8 0.3 collective-permute-done.8.refs_3_
  33.1 1.7 %collective-permute-start.9 = (bf16[512,128]{1,0:T(8,128)(2,1)S(1)}, bf16[512,128]{1,0:T(8,128)(2,1)S(1)}, u32[]{:S(2)}, u32[]{:S(2)}) collective-permute-start(bf16[512,128]{1,0:T(8,128)(2,1)S(1)} %slice.80.refs_0_), channel_id=1, source_target_pairs={{0,2},{2,4},{4,6},{6,0},{1,3},{3,5},{5,7},{7,1},{8,10},{10,12},{12... | collective-permute-start | bytes 393224 | tf_op jit(solution)/shard_map/ppermute | solution.py:242
  34.8 1.4 %collective-permute-done.7.refs_2_ = bf16[4,128,128]{2,1,0:T(8,128)(2,1)S(1)} collective-permute-done((bf16[4,128,128]{2,1,0:T(8,128)(2,1)S(1)}, bf16[4,128,128]{2,1,0:T(8,128)(2,1)S(1)}, u32[]{:S(2)}, u32[]{:S(2)}) %collective-permute-start.7) | collective-permute-done | bytes 131104 | tf_op jit(solution)/shard_map/ppermute | solution.py:242
  36.2 3.5 %collective-permute-start.14 = (bf16[4,32,1024]{2,1,0:T(8,128)(2,1)S(1)}, bf16[4,32,1024]{2,1,0:T(8,128)(2,1)S(1)}, u32[]{:S(2)}, u32[]{:S(2)}) collective-permute-start(bf16[4,32,1024]{2,1,0:T(8,128)(2,1)S(1)} %pad_maximum_fusion.refs_0_), channel_id=1, source_target_pairs={{0,24},{8,0},{16,8},{24,16},{32,56},{40,32},{48,40},{56,48},{64,88... | collective-permute-start | bytes 786440 | tf_op jit(solution)/shard_map/ppermute | solution.py:242
  39.7 0.0 collective-permute-done.6.refs_1_
  39.7 0.5 collective-permute-start.13
  40.3 0.0 copy-done.2
  40.3 0.1 copy-done.10
  40.4 9.3 %closure.1.x_ref = bf16[512,512]{1,0:T(8,128)(2,1)} custom-call(s32[4]{0:T(128)} %pad_add_fusion.index_ref, bf16[4,128,128]{2,1,0:T(8,128)(2,1)} %copy-done.2, bf16[4,128,128]{2,1,0:T(8,128)(2,1)} %copy-done.10, bf16[4,128,128]{2,1,0:T(8,128)(2,1)} %copy-done.9, bf16[4,128,128]{2,1,0:T(8,128)(2,1)} %copy-done.8), custom_call_target="tpu_custom_call" | custom-call | flops 10000000000 | bytes 2000000 | tf_op jit(solution)/shard_map/closure/pallas_call | solution.py:195
  49.7 0.0 collective-permute-done.11.refs_3_
  49.7 1.9 %collective-permute-start.12 = (bf16[4,32,1024]{2,1,0:T(8,128)(2,1)S(1)}, bf16[4,32,1024]{2,1,0:T(8,128)(2,1)S(1)}, u32[]{:S(2)}, u32[]{:S(2)}) collective-permute-start(bf16[4,32,1024]{2,1,0:T(8,128)(2,1)S(1)} %pad_maximum_fusion.refs_0_), channel_id=1, source_target_pairs={{0,8},{8,16},{16,24},{24,0},{32,40},{40,48},{48,56},{56,32},{64,72... | collective-permute-start | bytes 786440 | tf_op jit(solution)/shard_map/ppermute | solution.py:242
  51.6 0.0 collective-permute-done.10.refs_2_
  51.6 0.0 collective-permute-done.9.refs_1_
  51.6 0.6 copy-done.7
  52.3 0.7 copy-done.11
  52.9 5.2 %chain.1.own_ref = bf16[512,512]{1,0:T(8,128)(2,1)} custom-call(s32[4]{0:T(128)} %pad_add_fusion.index_ref, bf16[512,512]{1,0:T(8,128)(2,1)} %closure.1.x_ref, bf16[512,128]{1,0:T(8,128)(2,1)} %copy-done.1, bf16[512,128]{1,0:T(8,128)(2,1)} %copy-done.11, bf16[512,128]{1,0:T(8,128)(2,1)} %copy-done.7, bf16[512,128]{1,0:T(8,128)(2,1)} %copy-done.6), custom_call_target="tpu_custom_call" | custom-call | flops 4000000000 | bytes 2000000 | tf_op jit(solution)/shard_map/chain/pallas_call | solution.py:208
  58.1 0.0 collective-permute-done.14.refs_3_
  58.1 0.0 collective-permute-done.13.refs_2_
  58.1 0.0 copy-start.4
  58.2 0.0 collective-permute-done.12.refs_1_
  58.2 0.7 copy-done.3
  58.9 0.1 copy-done.4
  58.9 0.7 %copy-done.5 = bf16[4,32,1024]{2,1,0:T(8,128)(2,1)} copy-done((bf16[4,32,1024]{2,1,0:T(8,128)(2,1)}, bf16[4,32,1024]{2,1,0:T(8,128)(2,1)S(1)}, u32[]{:S(2)}) %copy-start.5) | copy-done | bytes 262168
  59.7 8.9 %final.1 = s32[512,1024]{1,0:T(8,128)} custom-call(s32[4]{0:T(128)} %pad_add_fusion.index_ref, bf16[512,512]{1,0:T(8,128)(2,1)} %chain.1.own_ref, bf16[4,32,1024]{2,1,0:T(8,128)(2,1)} %copy-done, bf16[4,32,1024]{2,1,0:T(8,128)(2,1)} %copy-done.5, bf16[4,32,1024]{2,1,0:T(8,128)(2,1)} %copy-done.4, bf16[4,32,1024]{2,1,0:T(8,128)(2,1)} %copy-done.3, ...), custom_call_target="tpu_custom_call" | custom-call | flops 4000000000 | bytes 2000000 | tf_op jit(solution)/shard_map/final/pallas_call | solution.py:221
  (36 shorter events, 0.3 us)
Async XLA Ops:
  3.9 45.8 %copy-start.1 = (bf16[512,128]{1,0:T(8,128)(2,1)}, bf16[512,128]{1,0:T(8,128)(2,1)S(1)}, u32[]{:S(2)}) copy-start(bf16[512,128]{1,0:T(8,128)(2,1)S(1)} %slice.80.refs_0_) | copy-start | bytes 393220
  3.9 45.8 %collective-permute-start.11 = (bf16[512,128]{1,0:T(8,128)(2,1)S(1)}, bf16[512,128]{1,0:T(8,128)(2,1)S(1)}, u32[]{:S(2)}, u32[]{:S(2)}) collective-permute-start(bf16[512,128]{1,0:T(8,128)(2,1)S(1)} %slice.80.refs_0_), channel_id=1, source_target_pairs={{0,6},{2,0},{4,2},{6,4},{1,7},{3,1},{5,3},{7,5},{8,14},{10,8},{12,... | collective-permute-start | bytes 393224 | tf_op jit(solution)/shard_map/ppermute | solution.py:242
  8.1 43.5 %collective-permute-start.10 = (bf16[512,128]{1,0:T(8,128)(2,1)S(1)}, bf16[512,128]{1,0:T(8,128)(2,1)S(1)}, u32[]{:S(2)}, u32[]{:S(2)}) collective-permute-start(bf16[512,128]{1,0:T(8,128)(2,1)S(1)} %slice.80.refs_0_), channel_id=1, source_target_pairs={{0,4},{2,6},{4,0},{6,2},{1,5},{3,7},{5,1},{7,3},{8,12},{10,14},{12... | collective-permute-start | bytes 393224 | tf_op jit(solution)/shard_map/ppermute | solution.py:242
  8.2 7.7 %collective-permute-start.2 = (bf16[48,1024]{1,0:T(8,128)(2,1)S(1)}, bf16[48,1024]{1,0:T(8,128)(2,1)S(1)}, u32[]{:S(2)}, u32[]{:S(2)}) collective-permute-start(bf16[48,1024]{1,0:T(8,128)(2,1)S(1)} %get-tuple-element.9), channel_id=1, source_target_pairs={{0,8},{32,40},{64,72},{96,104},{1,9},{33,41},{65,73},{97,105},{2,1... | collective-permute-start | bytes 294920 | tf_op jit(solution)/shard_map/ppermute | solution.py:257
  11.7 4.5 %collective-permute-start.1 = (bf16[48,1024]{1,0:T(8,128)(2,1)S(1)}, bf16[48,1024]{1,0:T(8,128)(2,1)S(1)}, u32[]{:S(2)}, u32[]{:S(2)}) collective-permute-start(bf16[48,1024]{1,0:T(8,128)(2,1)S(1)} %get-tuple-element.10), channel_id=1, source_target_pairs={{0,16},{32,48},{64,80},{96,112},{1,17},{33,49},{65,81},{97,113},{2... | collective-permute-start | bytes 294920 | tf_op jit(solution)/shard_map/ppermute | solution.py:257
  14.0 3.5 %collective-permute-start = (bf16[48,1024]{1,0:T(8,128)(2,1)S(1)}, bf16[48,1024]{1,0:T(8,128)(2,1)S(1)}, u32[]{:S(2)}, u32[]{:S(2)}) collective-permute-start(bf16[48,1024]{1,0:T(8,128)(2,1)S(1)} %get-tuple-element.11), channel_id=1, source_target_pairs={{0,24},{32,56},{64,88},{96,120},{1,25},{33,57},{65,89},{97,121},{2... | collective-permute-start | bytes 294920 | tf_op jit(solution)/shard_map/ppermute | solution.py:257
  17.6 6.5 %collective-permute-start.5 = (bf16[48,1024]{1,0:T(8,128)(2,1)S(1)}, bf16[48,1024]{1,0:T(8,128)(2,1)S(1)}, u32[]{:S(2)}, u32[]{:S(2)}) collective-permute-start(bf16[48,1024]{1,0:T(8,128)(2,1)S(1)} %fusion.2), channel_id=1, source_target_pairs={{0,96},{32,0},{64,32},{96,64},{8,104},{40,8},{72,40},{104,72},{16,... | collective-permute-start | bytes 294920 | tf_op jit(solution)/shard_map/ppermute | solution.py:242
  20.4 6.2 %collective-permute-start.4 = (bf16[48,1024]{1,0:T(8,128)(2,1)S(1)}, bf16[48,1024]{1,0:T(8,128)(2,1)S(1)}, u32[]{:S(2)}, u32[]{:S(2)}) collective-permute-start(bf16[48,1024]{1,0:T(8,128)(2,1)S(1)} %fusion.2), channel_id=1, source_target_pairs={{0,64},{32,96},{64,0},{96,32},{8,72},{40,104},{72,8},{104,40},{16,... | collective-permute-start | bytes 294920 | tf_op jit(solution)/shard_map/ppermute | solution.py:242
  21.2 6.4 %collective-permute-start.3 = (bf16[48,1024]{1,0:T(8,128)(2,1)S(1)}, bf16[48,1024]{1,0:T(8,128)(2,1)S(1)}, u32[]{:S(2)}, u32[]{:S(2)}) collective-permute-start(bf16[48,1024]{1,0:T(8,128)(2,1)S(1)} %fusion.2), channel_id=1, source_target_pairs={{0,32},{32,64},{64,96},{96,0},{8,40},{40,72},{72,104},{104,8},{16,... | collective-permute-start | bytes 294920 | tf_op jit(solution)/shard_map/ppermute | solution.py:242
  27.7 12.6 %copy-start.2 = (bf16[4,128,128]{2,1,0:T(8,128)(2,1)}, bf16[4,128,128]{2,1,0:T(8,128)(2,1)S(1)}, u32[]{:S(2)}) copy-start(bf16[4,128,128]{2,1,0:T(8,128)(2,1)S(1)} %constant_dynamic-update-slice_fusion.refs_0_) | copy-start | bytes 393220
  27.7 5.4 %collective-permute-start.8 = (bf16[4,128,128]{2,1,0:T(8,128)(2,1)S(1)}, bf16[4,128,128]{2,1,0:T(8,128)(2,1)S(1)}, u32[]{:S(2)}, u32[]{:S(2)}) collective-permute-start(bf16[4,128,128]{2,1,0:T(8,128)(2,1)S(1)} %constant_dynamic-update-slice_fusion.refs_0_), channel_id=1, source_target_pairs={{0,6},{2,0},{4,2},{6,4},{1,7},{3,1},{5,3},{7,5},{8,14},{10,8},{12,... | collective-permute-start | bytes 393224 | tf_op jit(solution)/shard_map/ppermute | solution.py:242
  28.4 7.8 %collective-permute-start.7 = (bf16[4,128,128]{2,1,0:T(8,128)(2,1)S(1)}, bf16[4,128,128]{2,1,0:T(8,128)(2,1)S(1)}, u32[]{:S(2)}, u32[]{:S(2)}) collective-permute-start(bf16[4,128,128]{2,1,0:T(8,128)(2,1)S(1)} %constant_dynamic-update-slice_fusion.refs_0_), channel_id=1, source_target_pairs={{0,4},{2,6},{4,0},{6,2},{1,5},{3,7},{5,1},{7,3},{8,12},{10,14},{12... | collective-permute-start | bytes 393224 | tf_op jit(solution)/shard_map/ppermute | solution.py:242
  31.4 8.4 %collective-permute-start.6 = (bf16[4,128,128]{2,1,0:T(8,128)(2,1)S(1)}, bf16[4,128,128]{2,1,0:T(8,128)(2,1)S(1)}, u32[]{:S(2)}, u32[]{:S(2)}) collective-permute-start(bf16[4,128,128]{2,1,0:T(8,128)(2,1)S(1)} %constant_dynamic-update-slice_fusion.refs_0_), channel_id=1, source_target_pairs={{0,2},{2,4},{4,6},{6,0},{1,3},{3,5},{5,7},{7,1},{8,10},{10,12},{12... | collective-permute-start | bytes 393224 | tf_op jit(solution)/shard_map/ppermute | solution.py:242
  32.8 16.9 %copy-start = (bf16[4,32,1024]{2,1,0:T(8,128)(2,1)}, bf16[4,32,1024]{2,1,0:T(8,128)(2,1)S(1)}, u32[]{:S(2)}) copy-start(bf16[4,32,1024]{2,1,0:T(8,128)(2,1)S(1)} %pad_maximum_fusion.refs_0_) | copy-start | bytes 786436
  33.1 7.2 %copy-start.8 = (bf16[4,128,128]{2,1,0:T(8,128)(2,1)}, bf16[4,128,128]{2,1,0:T(8,128)(2,1)S(1)}, u32[]{:S(2)}) copy-start(bf16[4,128,128]{2,1,0:T(8,128)(2,1)S(1)} %collective-permute-done.8.refs_3_) | copy-start | bytes 393220
  33.1 18.5 %collective-permute-start.9 = (bf16[512,128]{1,0:T(8,128)(2,1)S(1)}, bf16[512,128]{1,0:T(8,128)(2,1)S(1)}, u32[]{:S(2)}, u32[]{:S(2)}) collective-permute-start(bf16[512,128]{1,0:T(8,128)(2,1)S(1)} %slice.80.refs_0_), channel_id=1, source_target_pairs={{0,2},{2,4},{4,6},{6,0},{1,3},{3,5},{5,7},{7,1},{8,10},{10,12},{12... | collective-permute-start | bytes 393224 | tf_op jit(solution)/shard_map/ppermute | solution.py:242
  36.2 4.1 %copy-start.9 = (bf16[4,128,128]{2,1,0:T(8,128)(2,1)}, bf16[4,128,128]{2,1,0:T(8,128)(2,1)S(1)}, u32[]{:S(2)}) copy-start(bf16[4,128,128]{2,1,0:T(8,128)(2,1)S(1)} %collective-permute-done.7.refs_2_) | copy-start | bytes 393220
  36.2 21.9 %collective-permute-start.14 = (bf16[4,32,1024]{2,1,0:T(8,128)(2,1)S(1)}, bf16[4,32,1024]{2,1,0:T(8,128)(2,1)S(1)}, u32[]{:S(2)}, u32[]{:S(2)}) collective-permute-start(bf16[4,32,1024]{2,1,0:T(8,128)(2,1)S(1)} %pad_maximum_fusion.refs_0_), channel_id=1, source_target_pairs={{0,24},{8,0},{16,8},{24,16},{32,56},{40,32},{48,40},{56,48},{64,88... | collective-permute-start | bytes 786440 | tf_op jit(solution)/shard_map/ppermute | solution.py:242
  39.7 0.6 copy-start.10
  39.7 18.4 %collective-permute-start.13 = (bf16[4,32,1024]{2,1,0:T(8,128)(2,1)S(1)}, bf16[4,32,1024]{2,1,0:T(8,128)(2,1)S(1)}, u32[]{:S(2)}, u32[]{:S(2)}) collective-permute-start(bf16[4,32,1024]{2,1,0:T(8,128)(2,1)S(1)} %pad_maximum_fusion.refs_0_), channel_id=1, source_target_pairs={{0,16},{8,24},{16,0},{24,8},{32,48},{40,56},{48,32},{56,40},{64,80... | collective-permute-start | bytes 786440 | tf_op jit(solution)/shard_map/ppermute | solution.py:242
  49.7 1.9 %copy-start.6 = (bf16[512,128]{1,0:T(8,128)(2,1)}, bf16[512,128]{1,0:T(8,128)(2,1)S(1)}, u32[]{:S(2)}) copy-start(bf16[512,128]{1,0:T(8,128)(2,1)S(1)} %collective-permute-done.11.refs_3_) | copy-start | bytes 393220
  49.7 8.4 %collective-permute-start.12 = (bf16[4,32,1024]{2,1,0:T(8,128)(2,1)S(1)}, bf16[4,32,1024]{2,1,0:T(8,128)(2,1)S(1)}, u32[]{:S(2)}, u32[]{:S(2)}) collective-permute-start(bf16[4,32,1024]{2,1,0:T(8,128)(2,1)S(1)} %pad_maximum_fusion.refs_0_), channel_id=1, source_target_pairs={{0,8},{8,16},{16,24},{24,0},{32,40},{40,48},{48,56},{56,32},{64,72... | collective-permute-start | bytes 786440 | tf_op jit(solution)/shard_map/ppermute | solution.py:242
  51.6 0.6 copy-start.7
  52.3 0.7 copy-start.11
  58.1 0.7 %copy-start.3 = (bf16[4,32,1024]{2,1,0:T(8,128)(2,1)}, bf16[4,32,1024]{2,1,0:T(8,128)(2,1)S(1)}, u32[]{:S(2)}) copy-start(bf16[4,32,1024]{2,1,0:T(8,128)(2,1)S(1)} %collective-permute-done.14.refs_3_) | copy-start | bytes 786436
  58.1 0.8 %copy-start.4 = (bf16[4,32,1024]{2,1,0:T(8,128)(2,1)}, bf16[4,32,1024]{2,1,0:T(8,128)(2,1)S(1)}, u32[]{:S(2)}) copy-start(bf16[4,32,1024]{2,1,0:T(8,128)(2,1)S(1)} %collective-permute-done.13.refs_2_) | copy-start | bytes 786436
  58.9 0.7 %copy-start.5 = (bf16[4,32,1024]{2,1,0:T(8,128)(2,1)}, bf16[4,32,1024]{2,1,0:T(8,128)(2,1)S(1)}, u32[]{:S(2)}) copy-start(bf16[4,32,1024]{2,1,0:T(8,128)(2,1)S(1)} %collective-permute-done.12.refs_1_) | copy-start | bytes 786436

commit v2 on v1

v2 whole, which is shorter than its diff:
```python
import jax
import jax.numpy as jnp
from jax import lax
from jax.experimental import pallas as pl
from jax.experimental.pallas import tpu as pltpu
from jax.sharding import PartitionSpec as P

PIVOT = 128
STEPS = 4
SIDE = 4
HALF = 2 * PIVOT
SIZE = STEPS * PIVOT
PART = PIVOT // SIDE
F32, BF16 = jnp.float32, jnp.bfloat16
RATE = 8.0625
LN2 = 0.6931471805599453
SLACK = 0.004
TABLES = 6
SQUARINGS = 6
LINE = [[SIDE * i + k for k in range(SIDE)] for i in range(SIDE)]
COLUMN = [[SIDE * k + i for k in range(SIDE)] for i in range(SIDE)]
COL_LINE = [[2 * k + c for k in range(SIDE)] for c in range(2)]
PAIR = [[2 * k, 2 * k + 1] for k in range(SIDE)]


def encode(value):
    far = value >= BF16(33.0)
    a = value - jnp.where(far, BF16(33.0), BF16(1.0))
    scale = jnp.exp2(BF16(125.0) - BF16(8.0) * a) * jnp.exp2(BF16(-0.0625) * a)
    zero = jnp.zeros_like(scale)
    lo = jnp.where(far, zero, scale)
    t5 = jnp.where(far, scale * BF16(2.0**-12), zero)
    mid = jnp.where(value >= BF16(17.0), lo, zero)
    t1 = lo * BF16(2.0**-66)
    t4 = t1 * BF16(2.0**-62)
    t3 = t5 * BF16(2.0**-118)
    return t1, lo, t3, t4, t5, mid * BF16(2.0**123)


def decode(s1, s2, s3):
    near = s1 >= 2.0**-59.4
    middle = s2 >= 2.0**-121
    s = jnp.where(near, s1, jnp.where(middle, s2, s3))
    p1, p2, p3 = (p / RATE - SLACK + 2.0 for p in (118.0, 250.0, 496.0))
    p = jnp.where(near, p1, jnp.where(middle, p2, p3))
    return jnp.ceil(p - jnp.log(s) * (1.0 / (RATE * LN2)))


def dot(left, right):
    return jnp.dot(left, right, preferred_element_type=F32)


CHUNK = 32


def sums(left, right, rows, cols):
    def l(*tables):
        return jnp.concatenate([left[t, rows, :] for t in tables], axis=1)

    def r(*tables):
        return jnp.concatenate([right[t, :, cols] for t in tables], axis=0)

    return dot(l(0), r(0)), dot(l(3, 2, 1), r(2, 3, 1)), dot(l(1, 4, 5), r(4, 1, 5))


def lower(ref, rows, cols, windows):
    for i in range(0, windows[0].shape[0], CHUNK):
        at = slice(rows + i, rows + i + CHUNK)
        new = decode(*(w[i : i + CHUNK] for w in windows))
        ref[at, cols] = jnp.minimum(ref[at, cols].astype(F32), new).astype(BF16)


def encode_rows(ref, rows, cols, count, to):
    for i in range(0, count, CHUNK):
        for t, table in enumerate(encode(ref[rows + i : rows + i + CHUNK, cols])):
            to[t, i : i + CHUNK, :] = table


ALL = slice(0, HALF)
P_, Q_ = slice(0, HALF), slice(HALF, SIZE)


def close(x_ref, at, tab_ref):
    cols = slice(at, at + HALF)

    def square(_, carry):
        encode_rows(x_ref, at, cols, HALF, tab_ref)
        lower(x_ref, at, cols, sums(tab_ref, tab_ref, ALL, ALL))
        return carry

    lax.fori_loop(0, SQUARINGS, square, 0)
    encode_rows(x_ref, at, cols, HALF, tab_ref)


def multiply(ref, cols, source, source_cols, left_ref, right_ref, first, count):
    for n, r in enumerate(range(first, first + count, HALF)):
        left = left_ref.at[n]
        encode_rows(source, r, source_cols, HALF, left)
        lower(ref, r, cols, sums(left, right_ref, ALL, ALL))


def place(shift, axis_position):
    return pl.multiple_of(lax.rem(axis_position + SIDE - shift, SIDE) * PIVOT, PIVOT)


def chain_kernel(*refs):
    blocks, panels = refs[:SIDE], refs[SIDE : 2 * SIDE]
    own_ref, x_ref, left_ref, right_ref, tab_ref, block_sem, panel_sem = refs[2 * SIDE :]
    rows = own_ref.shape[0]
    ix, iz = lax.axis_index("row") // SIDE, lax.axis_index("col") // 2
    block_copies, panel_copies = [], []
    for shift in range(SIDE):
        col = pl.ds(place(shift, iz), PIVOT)
        for other in range(SIDE):
            to = x_ref.at[pl.ds(place(other, ix), PIVOT), col]
            block_copies.append(pltpu.make_async_copy(blocks[shift].at[other], to, block_sem.at[shift, other]))
        panel_copies.append(pltpu.make_async_copy(panels[shift], own_ref.at[:, col], panel_sem.at[shift]))
    for copy in block_copies + panel_copies:
        copy.start()
    for copy in block_copies:
        copy.wait()
    close(x_ref, 0, tab_ref)
    multiply(x_ref, P_, x_ref, P_, left_ref, tab_ref, HALF, HALF)
    encode_rows(x_ref, 0, Q_, HALF, right_ref)
    multiply(x_ref, Q_, x_ref, P_, left_ref, right_ref, HALF, HALF)
    for copy in panel_copies:
        copy.wait()
    multiply(own_ref, P_, own_ref, P_, left_ref, tab_ref, 0, rows)
    multiply(own_ref, Q_, own_ref, P_, left_ref, right_ref, 0, rows)
    close(x_ref, HALF, tab_ref)
    multiply(own_ref, Q_, own_ref, Q_, left_ref, tab_ref, 0, rows)
    encode_rows(x_ref, HALF, P_, HALF, right_ref)
    multiply(own_ref, P_, own_ref, Q_, left_ref, right_ref, 0, rows)


def final_kernel(own_ref, *refs):
    pieces = refs[:SIDE]
    weights_hbm, out_hbm, left_ref, right_ref, pivot_ref, sums_ref, weights_ref, out_ref, sem, in_sem, out_sem = refs[SIDE:]
    rows, total = weights_ref.shape
    row, col = lax.axis_index("row"), lax.axis_index("col")
    tiles = [slice(c, c + HALF) for c in range(0, total, HALF)]
    copies, loads, stores = [], [], []
    for shift in range(SIDE):
        q = lax.rem(row % SIDE + SIDE - shift, SIDE) * PART
        for other in range(SIDE):
            at = pl.multiple_of(place(other, row // SIDE) + q, PART)
            to = pivot_ref.at[pl.ds(at, PART), :]
            copies.append(pltpu.make_async_copy(pieces[shift].at[other], to, sem.at[shift, other]))
    for n, cols in enumerate(tiles):
        loads.append(pltpu.make_async_copy(weights_hbm.at[:, cols], weights_ref.at[:, cols], in_sem.at[n]))
        stores.append(pltpu.make_async_copy(out_ref.at[:, cols], out_hbm.at[:, cols], out_sem.at[n]))
    for copy in copies + loads:
        copy.start()
    for chunk in range(2):
        encode_rows(own_ref, 0, slice(chunk * HALF, (chunk + 1) * HALF), rows, left_ref.at[chunk])
    for copy in copies:
        copy.wait()

    def finish(n, r, slot):
        if r == 0:
            loads[n].wait()
        diagonal = row * rows + r - col * total - tiles[n].start
        for i in range(0, HALF, CHUNK):
            at, to = slice(i, i + CHUNK), slice(r + i, r + i + CHUNK)
            new = decode(*(jnp.maximum(sums_ref[slot, 0, w, at, :], sums_ref[slot, 1, w, at, :]) for w in range(3)))
            best = jnp.minimum(weights_ref[to, tiles[n]].astype(F32), new).astype(jnp.int32)
            down = lax.broadcasted_iota(jnp.int32, best.shape, 0)
            across = lax.broadcasted_iota(jnp.int32, best.shape, 1)
            out_ref[to, tiles[n]] = jnp.where(across - down == diagonal + i, 0, best)
        if r + HALF == rows:
            stores[n].start()

    units = [(n, r) for n in range(len(tiles)) for r in range(0, rows, HALF)]
    for u, (n, r) in enumerate(units):
        if r == 0:
            for chunk in range(2):
                encode_rows(pivot_ref, chunk * HALF, tiles[n], HALF, right_ref.at[n % 2, chunk])
        for chunk in range(2):
            at = slice(r, r + HALF)
            for w, value in enumerate(sums(left_ref.at[chunk], right_ref.at[n % 2, chunk], at, ALL)):
                sums_ref[u % 2, chunk, w] = value
        if u:
            finish(*units[u - 1], (u - 1) % 2)
    finish(*units[-1], (len(units) - 1) % 2)
    for copy in stores:
        copy.wait()


VMEM = pl.BlockSpec(memory_space=pltpu.VMEM)
ANY = pl.BlockSpec(memory_space=pl.ANY)


def cost(flops):
    return pl.CostEstimate(flops=flops, bytes_accessed=2_000_000, transcendentals=0)


def chain_call(blocks, panels):
    rows = panels[0].shape[0]
    return pl.pallas_call(
        chain_kernel,
        out_shape=jax.ShapeDtypeStruct((rows, SIZE), BF16),
        in_specs=[ANY] * (2 * SIDE),
        out_specs=VMEM,
        scratch_shapes=[
            pltpu.VMEM((SIZE, SIZE), BF16),
            pltpu.VMEM((rows // HALF, TABLES, HALF, HALF), BF16),
            pltpu.VMEM((TABLES, HALF, HALF), BF16),
            pltpu.VMEM((TABLES, HALF, HALF), BF16),
            pltpu.SemaphoreType.DMA((SIDE, SIDE)),
            pltpu.SemaphoreType.DMA((SIDE,)),
        ],
        compiler_params=pltpu.CompilerParams(vmem_limit_bytes=16 << 20),
        cost_estimate=cost(14_000_000_000),
        name="chain",
    )(*blocks, *panels)


def final_call(own, pieces, weights):
    rows, cols = weights.shape
    tiles = cols // HALF
    return pl.pallas_call(
        final_kernel,
        out_shape=jax.ShapeDtypeStruct((rows, cols), jnp.int32),
        in_specs=[VMEM] + [ANY] * (SIDE + 1),
        out_specs=ANY,
        scratch_shapes=[
            pltpu.VMEM((2, TABLES, rows, HALF), BF16),
            pltpu.VMEM((2, 2, TABLES, HALF, HALF), BF16),
            pltpu.VMEM((SIZE, cols), BF16),
            pltpu.VMEM((2, 2, 3, HALF, HALF), F32),
            pltpu.VMEM((rows, cols), jnp.int32),
            pltpu.VMEM((rows, cols), jnp.int32),
            pltpu.SemaphoreType.DMA((SIDE, SIDE)),
            pltpu.SemaphoreType.DMA((tiles,)),
            pltpu.SemaphoreType.DMA((tiles,)),
        ],
        compiler_params=pltpu.CompilerParams(vmem_limit_bytes=28 << 20),
        cost_estimate=cost(4_000_000_000),
        name="final",
    )(own, *pieces, weights)


def gather_line(array, axis, lines):
    got = {0: array}
    for shift in (1, 3, 2):
        pairs = [(line[i], line[(i + shift) % SIDE]) for line in lines for i in range(SIDE)]
        got[shift] = lax.ppermute(array, axis, pairs)
    return [got[shift] for shift in range(SIDE)]


def per_device(weights):
    _, cols = weights.shape
    row = lax.axis_index("row")
    panel = weights[:, :PIVOT].astype(BF16)
    strip = weights[:PIVOT, :].astype(BF16)
    panel = lax.all_gather(panel, "col", axis_index_groups=PAIR)[0]
    block = panel[:PIVOT].reshape(SIDE * SIDE, cols)
    message = jnp.concatenate([strip[:PART], block])
    for y in range(1, SIDE):
        sent = jnp.concatenate([strip[y * PART : (y + 1) * PART], block])
        got = lax.ppermute(sent, "row", [(line[0], line[y]) for line in LINE])
        message = jnp.where(row % SIDE == y, got, message)
    panels = gather_line(panel, "col", COL_LINE)
    along_x = gather_line(message, "row", COLUMN)
    quarters = jnp.stack([m[:PART] for m in along_x])
    blocks = jnp.stack([m[PART:].reshape(PIVOT, PIVOT) for m in along_x])
    blocks = gather_line(blocks, "col", COL_LINE)
    pieces = gather_line(quarters, "row", LINE)
    own = chain_call(blocks, panels)
    return final_call(own, pieces, weights)


def solution(mesh):
    placed = (P("row", "col"),)
    return jax.shard_map(
        per_device, mesh=mesh, in_specs=placed, out_specs=P("row", "col"), check_vma=False
    )
```

time: 68.8 us -> 56.6 us (0.82)
  the two profiles are of different devices: /device:TPU:0 before, /device:TPU:24 now
where the time goes in v2:
time: 56.6 us; the launch traced here: 56.4 us
  starting transfers between devices  22 us (39%)
  Pallas kernels  20.1 us (36%)
  waiting for transfers between devices  9.81 us (17%)
  blocking collectives  1.99 us (4%)
  other arithmetic  1.95 us (3%)
    ppermute x12, starting transfers between devices, gather_line(): got[shift] = lax.ppermute(array, axis, pairs)  19.4 us
    pallas_call x1, Pallas kernels, chain_call(): pl.pallas_call(chain_kernel, out_shape=jax.ShapeDtypeStruct((rows, SIZE),...  10.7 us
    pallas_call x1, Pallas kernels, final_call(): pl.pallas_call(final_kernel, out_shape=jax.ShapeDtypeStruct((rows, cols),...  9.32 us
    ppermute x12, waiting for transfers between devices, gather_line(): got[shift] = lax.ppermute(array, axis, pairs)  6.48 us
    ppermute x3, waiting for transfers between devices, per_device(): got = lax.ppermute(sent, 'row', [(line[0], line[y]) for line in LINE])  3.33 us
    ppermute x3, starting transfers between devices, per_device(): got = lax.ppermute(sent, 'row', [(line[0], line[y]) for line in LINE])  2.63 us
    all_gather x1, blocking collectives, per_device(): panel = lax.all_gather(panel, 'col', axis_index_groups=PAIR)[0]  1.99 us
    another operation x1, other arithmetic  1.84 us
  transfers between devices with their start and end apart: 15, of which 7 were waited for; matrix products, arithmetic and copies ran while one was open for 0% of the time, Pallas kernels for 19%

profile of v2, /device:TPU:24, one launch (start us, length us, event | category | flops | bytes accessed | tf_op | source)
XLA Modules:
  0.0 56.4 jit_solution(10274412336639745208)
XLA Ops:
  0.0 1.8 %convert.4 = bf16[512,1024]{1,0:T(8,128)(2,1)S(1)} convert(s32[512,1024]{1,0:T(8,128)} %refs_4_.1) | non-fusion elementwise | flops 524288 | bytes 3145728 | tf_op jit(solution)/shard_map/convert.1
  1.9 2.0 %all-gather = bf16[1024,128]{1,0:T(8,128)(2,1)S(1)} all-gather(bf16[512,128]{1,0:T(8,128)(2,1)S(1)} %slice.71), channel_id=2, replica_groups={{0,1},{2,3},{4,5},{6,7},{8,9},{10,11},{12,13},{14,15},{16,17},{18,19},{..., dimensions={0}, use_global_device_ids=true | all-gather | bytes 393216 | tf_op jit(solution)/shard_map/all_gather | solution.py:256
  4.0 0.7 %collective-permute-start.2 = (bf16[48,1024]{1,0:T(8,128)(2,1)S(1)}, bf16[48,1024]{1,0:T(8,128)(2,1)S(1)}, u32[]{:S(2)}, u32[]{:S(2)}) collective-permute-start(bf16[48,1024]{1,0:T(8,128)(2,1)S(1)} %get-tuple-element.9), channel_id=1, source_target_pairs={{0,8},{32,40},{64,72},{96,104},{1,9},{33,41},{65,73},{97,105},{2,1... | collective-permute-start | bytes 294920 | tf_op jit(solution)/shard_map/ppermute | solution.py:261
  4.6 0.7 %collective-permute-start.1 = (bf16[48,1024]{1,0:T(8,128)(2,1)S(1)}, bf16[48,1024]{1,0:T(8,128)(2,1)S(1)}, u32[]{:S(2)}, u32[]{:S(2)}) collective-permute-start(bf16[48,1024]{1,0:T(8,128)(2,1)S(1)} %get-tuple-element.10), channel_id=1, source_target_pairs={{0,16},{32,48},{64,80},{96,112},{1,17},{33,49},{65,81},{97,113},{2... | collective-permute-start | bytes 294920 | tf_op jit(solution)/shard_map/ppermute | solution.py:261
  5.3 1.3 %collective-permute-start = (bf16[48,1024]{1,0:T(8,128)(2,1)S(1)}, bf16[48,1024]{1,0:T(8,128)(2,1)S(1)}, u32[]{:S(2)}, u32[]{:S(2)}) collective-permute-start(bf16[48,1024]{1,0:T(8,128)(2,1)S(1)} %get-tuple-element.11), channel_id=1, source_target_pairs={{0,24},{32,56},{64,88},{96,120},{1,25},{33,57},{65,89},{97,121},{2... | collective-permute-start | bytes 294920 | tf_op jit(solution)/shard_map/ppermute | solution.py:261
  6.6 4.1 %collective-permute-start.11 = (bf16[512,128]{1,0:T(8,128)(2,1)S(1)}, bf16[512,128]{1,0:T(8,128)(2,1)S(1)}, u32[]{:S(2)}, u32[]{:S(2)}) collective-permute-start(bf16[512,128]{1,0:T(8,128)(2,1)S(1)} %slice.80.refs_4_), channel_id=1, source_target_pairs={{0,6},{2,0},{4,2},{6,4},{1,7},{3,1},{5,3},{7,5},{8,14},{10,8},{12,... | collective-permute-start | bytes 393224 | tf_op jit(solution)/shard_map/ppermute | solution.py:247
  10.7 0.0 collective-permute-start.10
  10.7 0.0 collective-permute-done.2
  10.7 0.0 collective-permute-done.1
  10.8 3.3 %collective-permute-done = bf16[48,1024]{1,0:T(8,128)(2,1)S(1)} collective-permute-done((bf16[48,1024]{1,0:T(8,128)(2,1)S(1)}, bf16[48,1024]{1,0:T(8,128)(2,1)S(1)}, u32[]{:S(2)}, u32[]{:S(2)}) %collective-permute-start) | collective-permute-done | bytes 98336 | tf_op jit(solution)/shard_map/ppermute | solution.py:261
  14.1 0.1 fusion.2
  14.2 2.8 %collective-permute-start.5 = (bf16[48,1024]{1,0:T(8,128)(2,1)S(1)}, bf16[48,1024]{1,0:T(8,128)(2,1)S(1)}, u32[]{:S(2)}, u32[]{:S(2)}) collective-permute-start(bf16[48,1024]{1,0:T(8,128)(2,1)S(1)} %fusion.2), channel_id=1, source_target_pairs={{0,96},{32,0},{64,32},{96,64},{8,104},{40,8},{72,40},{104,72},{16,... | collective-permute-start | bytes 294920 | tf_op jit(solution)/shard_map/ppermute | solution.py:247
  17.0 0.8 %collective-permute-start.4 = (bf16[48,1024]{1,0:T(8,128)(2,1)S(1)}, bf16[48,1024]{1,0:T(8,128)(2,1)S(1)}, u32[]{:S(2)}, u32[]{:S(2)}) collective-permute-start(bf16[48,1024]{1,0:T(8,128)(2,1)S(1)} %fusion.2), channel_id=1, source_target_pairs={{0,64},{32,96},{64,0},{96,32},{8,72},{40,104},{72,8},{104,40},{16,... | collective-permute-start | bytes 294920 | tf_op jit(solution)/shard_map/ppermute | solution.py:247
  17.8 0.9 %collective-permute-start.3 = (bf16[48,1024]{1,0:T(8,128)(2,1)S(1)}, bf16[48,1024]{1,0:T(8,128)(2,1)S(1)}, u32[]{:S(2)}, u32[]{:S(2)}) collective-permute-start(bf16[48,1024]{1,0:T(8,128)(2,1)S(1)} %fusion.2), channel_id=1, source_target_pairs={{0,32},{32,64},{64,96},{96,0},{8,40},{40,72},{72,104},{104,8},{16,... | collective-permute-start | bytes 294920 | tf_op jit(solution)/shard_map/ppermute | solution.py:247
  18.7 2.1 %collective-permute-done.5 = bf16[48,1024]{1,0:T(8,128)(2,1)S(1)} collective-permute-done((bf16[48,1024]{1,0:T(8,128)(2,1)S(1)}, bf16[48,1024]{1,0:T(8,128)(2,1)S(1)}, u32[]{:S(2)}, u32[]{:S(2)}) %collective-permute-start.5) | collective-permute-done | bytes 98336 | tf_op jit(solution)/shard_map/ppermute | solution.py:247
  20.8 1.9 %collective-permute-start.9 = (bf16[512,128]{1,0:T(8,128)(2,1)S(1)}, bf16[512,128]{1,0:T(8,128)(2,1)S(1)}, u32[]{:S(2)}, u32[]{:S(2)}) collective-permute-start(bf16[512,128]{1,0:T(8,128)(2,1)S(1)} %slice.80.refs_4_), channel_id=1, source_target_pairs={{0,2},{2,4},{4,6},{6,0},{1,3},{3,5},{5,7},{7,1},{8,10},{10,12},{12... | collective-permute-start | bytes 393224 | tf_op jit(solution)/shard_map/ppermute | solution.py:247
  22.8 0.5 collective-permute-done.4
  23.3 1.0 %collective-permute-done.3 = bf16[48,1024]{1,0:T(8,128)(2,1)S(1)} collective-permute-done((bf16[48,1024]{1,0:T(8,128)(2,1)S(1)}, bf16[48,1024]{1,0:T(8,128)(2,1)S(1)}, u32[]{:S(2)}, u32[]{:S(2)}) %collective-permute-start.3) | collective-permute-done | bytes 98336 | tf_op jit(solution)/shard_map/ppermute | solution.py:247
  24.4 4.1 %collective-permute-start.8 = (bf16[4,128,128]{2,1,0:T(8,128)(2,1)S(1)}, bf16[4,128,128]{2,1,0:T(8,128)(2,1)S(1)}, u32[]{:S(2)}, u32[]{:S(2)}) collective-permute-start(bf16[4,128,128]{2,1,0:T(8,128)(2,1)S(1)} %constant_dynamic-update-slice_fusion.refs_0_), channel_id=1, source_target_pairs={{0,6},{2,0},{4,2},{6,4},{1,7},{3,1},{5,3},{7,5},{8,14},{10,8},{12,... | collective-permute-start | bytes 393224 | tf_op jit(solution)/shard_map/ppermute | solution.py:247
  28.5 0.0 collective-permute-start.7
  28.5 0.0 collective-permute-done.11.refs_7_
  28.5 1.3 %collective-permute-start.6 = (bf16[4,128,128]{2,1,0:T(8,128)(2,1)S(1)}, bf16[4,128,128]{2,1,0:T(8,128)(2,1)S(1)}, u32[]{:S(2)}, u32[]{:S(2)}) collective-permute-start(bf16[4,128,128]{2,1,0:T(8,128)(2,1)S(1)} %constant_dynamic-update-slice_fusion.refs_0_), channel_id=1, source_target_pairs={{0,2},{2,4},{4,6},{6,0},{1,3},{3,5},{5,7},{7,1},{8,10},{10,12},{12... | collective-permute-start | bytes 393224 | tf_op jit(solution)/shard_map/ppermute | solution.py:247
  29.9 0.0 copy-start
  29.9 0.0 collective-permute-done.10.refs_6_
  29.9 0.1 collective-permute-start.14
  30.0 0.0 collective-permute-done.9.refs_5_
  30.0 2.5 %collective-permute-start.13 = (bf16[4,32,1024]{2,1,0:T(8,128)(2,1)S(1)}, bf16[4,32,1024]{2,1,0:T(8,128)(2,1)S(1)}, u32[]{:S(2)}, u32[]{:S(2)}) collective-permute-start(bf16[4,32,1024]{2,1,0:T(8,128)(2,1)S(1)} %pad_maximum_fusion.refs_0_), channel_id=1, source_target_pairs={{0,16},{8,24},{16,0},{24,8},{32,48},{40,56},{48,32},{56,40},{64,80... | collective-permute-start | bytes 786440 | tf_op jit(solution)/shard_map/ppermute | solution.py:247
  32.5 0.1 collective-permute-done.8.refs_3_
  32.6 0.9 %collective-permute-start.12 = (bf16[4,32,1024]{2,1,0:T(8,128)(2,1)S(1)}, bf16[4,32,1024]{2,1,0:T(8,128)(2,1)S(1)}, u32[]{:S(2)}, u32[]{:S(2)}) collective-permute-start(bf16[4,32,1024]{2,1,0:T(8,128)(2,1)S(1)} %pad_maximum_fusion.refs_0_), channel_id=1, source_target_pairs={{0,8},{8,16},{16,24},{24,0},{32,40},{40,48},{48,56},{56,32},{64,72... | collective-permute-start | bytes 786440 | tf_op jit(solution)/shard_map/ppermute | solution.py:247
  33.5 1.6 %collective-permute-done.7.refs_2_ = bf16[4,128,128]{2,1,0:T(8,128)(2,1)S(1)} collective-permute-done((bf16[4,128,128]{2,1,0:T(8,128)(2,1)S(1)}, bf16[4,128,128]{2,1,0:T(8,128)(2,1)S(1)}, u32[]{:S(2)}, u32[]{:S(2)}) %collective-permute-start.7) | collective-permute-done | bytes 131104 | tf_op jit(solution)/shard_map/ppermute | solution.py:247
  35.1 1.1 %collective-permute-done.6.refs_1_ = bf16[4,128,128]{2,1,0:T(8,128)(2,1)S(1)} collective-permute-done((bf16[4,128,128]{2,1,0:T(8,128)(2,1)S(1)}, bf16[4,128,128]{2,1,0:T(8,128)(2,1)S(1)}, u32[]{:S(2)}, u32[]{:S(2)}) %collective-permute-start.6) | collective-permute-done | bytes 131104 | tf_op jit(solution)/shard_map/ppermute | solution.py:247
  36.2 10.7 %chain.1.own_ref = bf16[512,512]{1,0:T(8,128)(2,1)S(1)} custom-call(bf16[4,128,128]{2,1,0:T(8,128)(2,1)S(1)} %constant_dynamic-update-slice_fusion.refs_0_, bf16[4,128,128]{2,1,0:T(8,128)(2,1)S(1)} %collective-permute-done.6.refs_1_, bf16[4,128,128]{2,1,0:T(8,128)(2,1)S(1)} %collective-permute-done.7.refs_2_, ...), custom_call_target="tpu_custom_call" | custom-call | flops 14000000000 | bytes 2000000 | tf_op jit(solution)/shard_map/chain/pallas_call | solution.py:199
  46.9 0.0 collective-permute-done.14.refs_3_
  46.9 0.0 collective-permute-done.13.refs_2_
  46.9 0.0 collective-permute-done.12.refs_1_
  47.0 0.0 copy-done
  47.0 9.3 %final.1 = s32[512,1024]{1,0:T(8,128)} custom-call(bf16[512,512]{1,0:T(8,128)(2,1)S(1)} %chain.1.own_ref, bf16[4,32,1024]{2,1,0:T(8,128)(2,1)S(1)} %pad_maximum_fusion.refs_0_, bf16[4,32,1024]{2,1,0:T(8,128)(2,1)S(1)} %collective-permute-done.12.refs_1_, bf16[4,32,1024]{2,1,0:T(8,128)(2,1)S(1)} %collective-permute-done.13.refs_2_, ...), custom_call_target="tpu_custom_call" | custom-call | flops 4000000000 | bytes 2000000 | tf_op jit(solution)/shard_map/final/pallas_call | solution.py:221
  (23 shorter events, 0.3 us)
Async XLA Ops:
  4.0 6.8 %collective-permute-start.2 = (bf16[48,1024]{1,0:T(8,128)(2,1)S(1)}, bf16[48,1024]{1,0:T(8,128)(2,1)S(1)}, u32[]{:S(2)}, u32[]{:S(2)}) collective-permute-start(bf16[48,1024]{1,0:T(8,128)(2,1)S(1)} %get-tuple-element.9), channel_id=1, source_target_pairs={{0,8},{32,40},{64,72},{96,104},{1,9},{33,41},{65,73},{97,105},{2,1... | collective-permute-start | bytes 294920 | tf_op jit(solution)/shard_map/ppermute | solution.py:261
  4.6 6.1 %collective-permute-start.1 = (bf16[48,1024]{1,0:T(8,128)(2,1)S(1)}, bf16[48,1024]{1,0:T(8,128)(2,1)S(1)}, u32[]{:S(2)}, u32[]{:S(2)}) collective-permute-start(bf16[48,1024]{1,0:T(8,128)(2,1)S(1)} %get-tuple-element.10), channel_id=1, source_target_pairs={{0,16},{32,48},{64,80},{96,112},{1,17},{33,49},{65,81},{97,113},{2... | collective-permute-start | bytes 294920 | tf_op jit(solution)/shard_map/ppermute | solution.py:261
  5.3 8.8 %collective-permute-start = (bf16[48,1024]{1,0:T(8,128)(2,1)S(1)}, bf16[48,1024]{1,0:T(8,128)(2,1)S(1)}, u32[]{:S(2)}, u32[]{:S(2)}) collective-permute-start(bf16[48,1024]{1,0:T(8,128)(2,1)S(1)} %get-tuple-element.11), channel_id=1, source_target_pairs={{0,24},{32,56},{64,88},{96,120},{1,25},{33,57},{65,89},{97,121},{2... | collective-permute-start | bytes 294920 | tf_op jit(solution)/shard_map/ppermute | solution.py:261
  6.6 21.9 %collective-permute-start.11 = (bf16[512,128]{1,0:T(8,128)(2,1)S(1)}, bf16[512,128]{1,0:T(8,128)(2,1)S(1)}, u32[]{:S(2)}, u32[]{:S(2)}) collective-permute-start(bf16[512,128]{1,0:T(8,128)(2,1)S(1)} %slice.80.refs_4_), channel_id=1, source_target_pairs={{0,6},{2,0},{4,2},{6,4},{1,7},{3,1},{5,3},{7,5},{8,14},{10,8},{12,... | collective-permute-start | bytes 393224 | tf_op jit(solution)/shard_map/ppermute | solution.py:247
  10.7 19.2 %collective-permute-start.10 = (bf16[512,128]{1,0:T(8,128)(2,1)S(1)}, bf16[512,128]{1,0:T(8,128)(2,1)S(1)}, u32[]{:S(2)}, u32[]{:S(2)}) collective-permute-start(bf16[512,128]{1,0:T(8,128)(2,1)S(1)} %slice.80.refs_4_), channel_id=1, source_target_pairs={{0,4},{2,6},{4,0},{6,2},{1,5},{3,7},{5,1},{7,3},{8,12},{10,14},{12... | collective-permute-start | bytes 393224 | tf_op jit(solution)/shard_map/ppermute | solution.py:247
  14.2 6.7 %collective-permute-start.5 = (bf16[48,1024]{1,0:T(8,128)(2,1)S(1)}, bf16[48,1024]{1,0:T(8,128)(2,1)S(1)}, u32[]{:S(2)}, u32[]{:S(2)}) collective-permute-start(bf16[48,1024]{1,0:T(8,128)(2,1)S(1)} %fusion.2), channel_id=1, source_target_pairs={{0,96},{32,0},{64,32},{96,64},{8,104},{40,8},{72,40},{104,72},{16,... | collective-permute-start | bytes 294920 | tf_op jit(solution)/shard_map/ppermute | solution.py:247
  17.0 6.3 %collective-permute-start.4 = (bf16[48,1024]{1,0:T(8,128)(2,1)S(1)}, bf16[48,1024]{1,0:T(8,128)(2,1)S(1)}, u32[]{:S(2)}, u32[]{:S(2)}) collective-permute-start(bf16[48,1024]{1,0:T(8,128)(2,1)S(1)} %fusion.2), channel_id=1, source_target_pairs={{0,64},{32,96},{64,0},{96,32},{8,72},{40,104},{72,8},{104,40},{16,... | collective-permute-start | bytes 294920 | tf_op jit(solution)/shard_map/ppermute | solution.py:247
  17.8 6.5 %collective-permute-start.3 = (bf16[48,1024]{1,0:T(8,128)(2,1)S(1)}, bf16[48,1024]{1,0:T(8,128)(2,1)S(1)}, u32[]{:S(2)}, u32[]{:S(2)}) collective-permute-start(bf16[48,1024]{1,0:T(8,128)(2,1)S(1)} %fusion.2), channel_id=1, source_target_pairs={{0,32},{32,64},{64,96},{96,0},{8,40},{40,72},{72,104},{104,8},{16,... | collective-permute-start | bytes 294920 | tf_op jit(solution)/shard_map/ppermute | solution.py:247
  20.8 9.1 %collective-permute-start.9 = (bf16[512,128]{1,0:T(8,128)(2,1)S(1)}, bf16[512,128]{1,0:T(8,128)(2,1)S(1)}, u32[]{:S(2)}, u32[]{:S(2)}) collective-permute-start(bf16[512,128]{1,0:T(8,128)(2,1)S(1)} %slice.80.refs_4_), channel_id=1, source_target_pairs={{0,2},{2,4},{4,6},{6,0},{1,3},{3,5},{5,7},{7,1},{8,10},{10,12},{12... | collective-permute-start | bytes 393224 | tf_op jit(solution)/shard_map/ppermute | solution.py:247
  24.4 8.2 %collective-permute-start.8 = (bf16[4,128,128]{2,1,0:T(8,128)(2,1)S(1)}, bf16[4,128,128]{2,1,0:T(8,128)(2,1)S(1)}, u32[]{:S(2)}, u32[]{:S(2)}) collective-permute-start(bf16[4,128,128]{2,1,0:T(8,128)(2,1)S(1)} %constant_dynamic-update-slice_fusion.refs_0_), channel_id=1, source_target_pairs={{0,6},{2,0},{4,2},{6,4},{1,7},{3,1},{5,3},{7,5},{8,14},{10,8},{12,... | collective-permute-start | bytes 393224 | tf_op jit(solution)/shard_map/ppermute | solution.py:247
  28.5 6.6 %collective-permute-start.7 = (bf16[4,128,128]{2,1,0:T(8,128)(2,1)S(1)}, bf16[4,128,128]{2,1,0:T(8,128)(2,1)S(1)}, u32[]{:S(2)}, u32[]{:S(2)}) collective-permute-start(bf16[4,128,128]{2,1,0:T(8,128)(2,1)S(1)} %constant_dynamic-update-slice_fusion.refs_0_), channel_id=1, source_target_pairs={{0,4},{2,6},{4,0},{6,2},{1,5},{3,7},{5,1},{7,3},{8,12},{10,14},{12... | collective-permute-start | bytes 393224 | tf_op jit(solution)/shard_map/ppermute | solution.py:247
  28.5 7.7 %collective-permute-start.6 = (bf16[4,128,128]{2,1,0:T(8,128)(2,1)S(1)}, bf16[4,128,128]{2,1,0:T(8,128)(2,1)S(1)}, u32[]{:S(2)}, u32[]{:S(2)}) collective-permute-start(bf16[4,128,128]{2,1,0:T(8,128)(2,1)S(1)} %constant_dynamic-update-slice_fusion.refs_0_), channel_id=1, source_target_pairs={{0,2},{2,4},{4,6},{6,0},{1,3},{3,5},{5,7},{7,1},{8,10},{10,12},{12... | collective-permute-start | bytes 393224 | tf_op jit(solution)/shard_map/ppermute | solution.py:247
  29.9 17.1 %copy-start = (s32[512,1024]{1,0:T(8,128)S(1)}, s32[512,1024]{1,0:T(8,128)}, u32[]{:S(2)}) copy-start(s32[512,1024]{1,0:T(8,128)} %refs_4_.1) | copy-start | bytes 6291460
  29.9 17.0 %collective-permute-start.14 = (bf16[4,32,1024]{2,1,0:T(8,128)(2,1)S(1)}, bf16[4,32,1024]{2,1,0:T(8,128)(2,1)S(1)}, u32[]{:S(2)}, u32[]{:S(2)}) collective-permute-start(bf16[4,32,1024]{2,1,0:T(8,128)(2,1)S(1)} %pad_maximum_fusion.refs_0_), channel_id=1, source_target_pairs={{0,24},{8,0},{16,8},{24,16},{32,56},{40,32},{48,40},{56,48},{64,88... | collective-permute-start | bytes 786440 | tf_op jit(solution)/shard_map/ppermute | solution.py:247
  30.0 16.9 %collective-permute-start.13 = (bf16[4,32,1024]{2,1,0:T(8,128)(2,1)S(1)}, bf16[4,32,1024]{2,1,0:T(8,128)(2,1)S(1)}, u32[]{:S(2)}, u32[]{:S(2)}) collective-permute-start(bf16[4,32,1024]{2,1,0:T(8,128)(2,1)S(1)} %pad_maximum_fusion.refs_0_), channel_id=1, source_target_pairs={{0,16},{8,24},{16,0},{24,8},{32,48},{40,56},{48,32},{56,40},{64,80... | collective-permute-start | bytes 786440 | tf_op jit(solution)/shard_map/ppermute | solution.py:247
  32.6 14.3 %collective-permute-start.12 = (bf16[4,32,1024]{2,1,0:T(8,128)(2,1)S(1)}, bf16[4,32,1024]{2,1,0:T(8,128)(2,1)S(1)}, u32[]{:S(2)}, u32[]{:S(2)}) collective-permute-start(bf16[4,32,1024]{2,1,0:T(8,128)(2,1)S(1)} %pad_maximum_fusion.refs_0_), channel_id=1, source_target_pairs={{0,8},{8,16},{16,24},{24,0},{32,40},{40,48},{48,56},{56,32},{64,72... | collective-permute-start | bytes 786440 | tf_op jit(solution)/shard_map/ppermute | solution.py:247

commit v3 on v2

v3 whole, which is shorter than its diff:
```python
import jax
import jax.numpy as jnp
from jax import lax
from jax.experimental import pallas as pl
from jax.experimental.pallas import tpu as pltpu
from jax.sharding import PartitionSpec as P

PIVOT = 128
STEPS = 4
SIDE = 4
HALF = 2 * PIVOT
SIZE = STEPS * PIVOT
F32, BF16 = jnp.float32, jnp.bfloat16
RATE = 8.0625
LN2 = 0.6931471805599453
SLACK = 0.004
TABLES = 6
SQUARINGS = 6
LINE = [[SIDE * i + k for k in range(SIDE)] for i in range(SIDE)]
COLUMN = [[SIDE * k + i for k in range(SIDE)] for i in range(SIDE)]
COL_LINE = [[2 * k + c for k in range(SIDE)] for c in range(2)]
PAIR = [[2 * k, 2 * k + 1] for k in range(SIDE)]


def encode(value):
    far = value >= BF16(33.0)
    a = value - jnp.where(far, BF16(33.0), BF16(1.0))
    scale = jnp.exp2(BF16(125.0) - BF16(8.0) * a) * jnp.exp2(BF16(-0.0625) * a)
    zero = jnp.zeros_like(scale)
    lo = jnp.where(far, zero, scale)
    t5 = jnp.where(far, scale * BF16(2.0**-12), zero)
    mid = jnp.where(value >= BF16(17.0), lo, zero)
    t1 = lo * BF16(2.0**-66)
    t4 = t1 * BF16(2.0**-62)
    t3 = t5 * BF16(2.0**-118)
    return t1, lo, t3, t4, t5, mid * BF16(2.0**123)


def decode(s1, s2, s3):
    near = s1 >= 2.0**-59.4
    middle = s2 >= 2.0**-121
    s = jnp.where(near, s1, jnp.where(middle, s2, s3))
    p1, p2, p3 = (p / RATE - SLACK + 2.0 for p in (118.0, 250.0, 496.0))
    p = jnp.where(near, p1, jnp.where(middle, p2, p3))
    return jnp.ceil(p - jnp.log(s) * (1.0 / (RATE * LN2)))


def dot(left, right):
    return jnp.dot(left, right, preferred_element_type=F32)


CHUNK = 32


def sums(left, right, rows, cols):
    def l(*tables):
        return jnp.concatenate([left[t, rows, :] for t in tables], axis=1)

    def r(*tables):
        return jnp.concatenate([right[t, :, cols] for t in tables], axis=0)

    return dot(l(0), r(0)), dot(l(3, 2, 1), r(2, 3, 1)), dot(l(1, 4, 5), r(4, 1, 5))


def lower(ref, rows, cols, windows):
    for i in range(0, windows[0].shape[0], CHUNK):
        at = slice(rows + i, rows + i + CHUNK)
        new = decode(*(w[i : i + CHUNK] for w in windows))
        ref[at, cols] = jnp.minimum(ref[at, cols].astype(F32), new).astype(BF16)


def encode_rows(ref, rows, cols, count, to, at=0):
    for i in range(0, count, CHUNK):
        for t, table in enumerate(encode(ref[rows + i : rows + i + CHUNK, cols])):
            to[t, at + i : at + i + CHUNK, :] = table


ALL = slice(0, HALF)
P_, Q_ = slice(0, HALF), slice(HALF, SIZE)


def square(x_ref, at, tab_ref):
    cols = slice(at, at + HALF)
    lower(x_ref, at, cols, sums(tab_ref, tab_ref, ALL, ALL))
    encode_rows(x_ref, at, cols, HALF, tab_ref)


def close(x_ref, at, tab_ref):
    def body(_, carry):
        square(x_ref, at, tab_ref)
        return carry

    encode_rows(x_ref, at, slice(at, at + HALF), HALF, tab_ref)
    lax.fori_loop(0, SQUARINGS, body, 0)


def multiply(ref, cols, source, source_cols, left, right_ref, r):
    encode_rows(source, r, source_cols, HALF, left)
    lower(ref, r, cols, sums(left, right_ref, ALL, ALL))


def chain_kernel(*refs):
    blocks, panels = refs[:SIDE], refs[SIDE : 2 * SIDE]
    own_ref, x_ref, left_ref, right_ref, tab_ref, block_sem, panel_sem = refs[2 * SIDE :]
    rows = own_ref.shape[0]
    first = lax.axis_index("row") // SIDE + 2 * SIDE - lax.axis_index("col") // 2
    block_copies, panel_copies = [], []
    for shift in range(SIDE):
        col = pl.ds(pl.multiple_of(lax.rem(first + shift, SIDE) * PIVOT, PIVOT), PIVOT)
        for other in range(SIDE):
            to = x_ref.at[other * PIVOT : (other + 1) * PIVOT, col]
            block_copies.append(pltpu.make_async_copy(blocks[shift].at[other], to, block_sem.at[shift, other]))
        panel_copies.append(pltpu.make_async_copy(panels[shift], own_ref.at[:, col], panel_sem.at[shift]))
    for copy in block_copies + panel_copies:
        copy.start()
    for copy in block_copies:
        copy.wait()
    halves = range(0, rows, HALF)
    close(x_ref, 0, tab_ref.at[0])
    multiply(x_ref, P_, x_ref, P_, left_ref.at[0], tab_ref.at[0], HALF)
    encode_rows(x_ref, 0, Q_, HALF, right_ref)
    multiply(x_ref, Q_, x_ref, P_, left_ref.at[1], right_ref, HALF)
    for copy in panel_copies:
        copy.wait()
    work = [(cols, table, r) for cols, table in ((P_, tab_ref.at[0]), (Q_, right_ref)) for r in halves]
    encode_rows(x_ref, HALF, Q_, HALF, tab_ref.at[1])
    for n in range(SQUARINGS):
        if n < len(work):
            cols, table, r = work[n]
            multiply(own_ref, cols, own_ref, P_, left_ref.at[n % 2], table, r)
        square(x_ref, HALF, tab_ref.at[1])
    for cols, table, r in work[SQUARINGS:]:
        multiply(own_ref, cols, own_ref, P_, left_ref.at[0], table, r)
    encode_rows(x_ref, HALF, P_, HALF, right_ref)
    for n, r in enumerate(halves):
        multiply(own_ref, Q_, own_ref, Q_, left_ref.at[n % 2], tab_ref.at[1], r)
    for n, r in enumerate(halves):
        multiply(own_ref, P_, own_ref, Q_, left_ref.at[n % 2], right_ref, r)


def final_kernel(own_ref, *refs):
    pieces = refs[:SIDE]
    weights_ref, out_hbm, left_ref, right_ref, sums_ref, out_ref, sem = refs[SIDE:]
    rows, total = weights_ref.shape
    row, col = lax.axis_index("row"), lax.axis_index("col")
    starts = [pl.multiple_of(lax.rem(row % SIDE + SIDE - n, SIDE) * HALF, HALF) for n in range(SIDE)]
    stores = [
        pltpu.make_async_copy(out_ref.at[n], out_hbm.at[:, pl.ds(starts[n], HALF)], sem.at[n]) for n in range(SIDE)
    ]
    for chunk in range(2):
        encode_rows(own_ref, 0, slice(chunk * HALF, (chunk + 1) * HALF), rows, left_ref.at[chunk])

    def finish(n, r, slot):
        diagonal = row * rows + r - col * total - starts[n]
        for i in range(0, HALF, CHUNK):
            at, to = slice(i, i + CHUNK), slice(r + i, r + i + CHUNK)
            new = decode(*(jnp.maximum(sums_ref[slot, 0, w, at, :], sums_ref[slot, 1, w, at, :]) for w in range(3)))
            old = weights_ref[to, pl.ds(starts[n], HALF)].astype(F32)
            best = jnp.minimum(old, new).astype(jnp.int32)
            down = lax.broadcasted_iota(jnp.int32, best.shape, 0)
            across = lax.broadcasted_iota(jnp.int32, best.shape, 1)
            out_ref[n, to, :] = jnp.where(across - down == diagonal + i, 0, best)
        if r + HALF == rows:
            stores[n].start()

    units = [(n, r) for n in range(SIDE) for r in range(0, rows, HALF)]
    for u, (n, r) in enumerate(units):
        if r == 0:
            for k in range(SIDE):
                encode_rows(pieces[n].at[k], 0, ALL, PIVOT, right_ref.at[n % 2, k // 2], (k % 2) * PIVOT)
        for chunk in range(2):
            at = slice(r, r + HALF)
            for w, value in enumerate(sums(left_ref.at[chunk], right_ref.at[n % 2, chunk], at, ALL)):
                sums_ref[u % 2, chunk, w] = value
        if u:
            finish(*units[u - 1], (u - 1) % 2)
    finish(*units[-1], (len(units) - 1) % 2)
    for copy in stores:
        copy.wait()


VMEM = pl.BlockSpec(memory_space=pltpu.VMEM)
ANY = pl.BlockSpec(memory_space=pl.ANY)


def cost(flops):
    return pl.CostEstimate(flops=flops, bytes_accessed=2_000_000, transcendentals=0)


def chain_call(blocks, panels):
    rows = panels[0].shape[0]
    return pl.pallas_call(
        chain_kernel,
        out_shape=jax.ShapeDtypeStruct((rows, SIZE), BF16),
        in_specs=[ANY] * (2 * SIDE),
        out_specs=VMEM,
        scratch_shapes=[
            pltpu.VMEM((SIZE, SIZE), BF16),
            pltpu.VMEM((2, TABLES, HALF, HALF), BF16),
            pltpu.VMEM((TABLES, HALF, HALF), BF16),
            pltpu.VMEM((2, TABLES, HALF, HALF), BF16),
            pltpu.SemaphoreType.DMA((SIDE, SIDE)),
            pltpu.SemaphoreType.DMA((SIDE,)),
        ],
        compiler_params=pltpu.CompilerParams(vmem_limit_bytes=16 << 20),
        cost_estimate=cost(14_000_000_000),
        name="chain",
    )(*blocks, *panels)


def final_call(own, pieces, weights):
    rows, cols = weights.shape
    return pl.pallas_call(
        final_kernel,
        out_shape=jax.ShapeDtypeStruct((rows, cols), jnp.int32),
        in_specs=[VMEM] * (SIDE + 2),
        out_specs=ANY,
        scratch_shapes=[
            pltpu.VMEM((2, TABLES, rows, HALF), BF16),
            pltpu.VMEM((2, 2, TABLES, HALF, HALF), BF16),
            pltpu.VMEM((2, 2, 3, HALF, HALF), F32),
            pltpu.VMEM((SIDE, rows, HALF), jnp.int32),
            pltpu.SemaphoreType.DMA((SIDE,)),
        ],
        compiler_params=pltpu.CompilerParams(vmem_limit_bytes=28 << 20),
        cost_estimate=cost(4_000_000_000),
        name="final",
    )(own, *pieces, weights)


def gather_line(array, axis, lines):
    got = {0: array}
    for shift in (1, 3, 2):
        pairs = [(line[i], line[(i + shift) % SIDE]) for line in lines for i in range(SIDE)]
        got[shift] = lax.ppermute(array, axis, pairs)
    return [got[shift] for shift in range(SIDE)]


def per_device(weights):
    row = lax.axis_index("row")
    strip = lax.optimization_barrier(weights[:PIVOT, :]).astype(BF16)
    block = lax.all_gather(strip[:, :PIVOT], "col", axis_index_groups=PAIR)[0]
    panel = lax.optimization_barrier(weights[:, :PIVOT]).astype(BF16)
    panel = lax.all_gather(panel, "col", axis_index_groups=PAIR)[0]
    message = jnp.concatenate([strip[:, :HALF], block], axis=1)
    for y in range(1, SIDE):
        sent = jnp.concatenate([strip[:, y * HALF : (y + 1) * HALF], block], axis=1)
        got = lax.ppermute(sent, "row", [(line[0], line[y]) for line in LINE])
        message = jnp.where(row % SIDE == y, got, message)
    panels = gather_line(panel, "col", COL_LINE)
    along_x = gather_line(message, "row", COLUMN)
    quarters = jnp.stack([m[:, :HALF] for m in along_x])
    blocks = jnp.stack([m[:, HALF:] for m in along_x])
    blocks = gather_line(blocks, "col", COL_LINE)
    pieces = gather_line(quarters, "row", LINE)
    own = chain_call(blocks, panels)
    return final_call(own, pieces, weights)


def solution(mesh):
    placed = (P("row", "col"),)
    return jax.shard_map(
        per_device, mesh=mesh, in_specs=placed, out_specs=P("row", "col"), check_vma=False
    )
```

time: 56.6 us -> 57.7 us (1.019)
  the two profiles are of different devices: /device:TPU:24 before, /device:TPU:0 now
where the time goes in v3:
time: 57.7 us; the launch traced here: 57.5 us
  starting transfers between devices  23 us (40%)
  Pallas kernels  15.8 us (27%)
  waiting for transfers between devices  13 us (23%)
  blocking collectives  3.85 us (7%)
  local copies, waits for them, and re-layouts  1.24 us (2%)
    ppermute x12, starting transfers between devices, gather_line(): got[shift] = lax.ppermute(array, axis, pairs)  15.8 us
    ppermute x12, waiting for transfers between devices, gather_line(): got[shift] = lax.ppermute(array, axis, pairs)  13 us
    pallas_call x1, Pallas kernels, chain_call(): pl.pallas_call(chain_kernel, out_shape=jax.ShapeDtypeStruct((rows, SIZE),...  10.1 us
    ppermute x3, starting transfers between devices, per_device(): got = lax.ppermute(sent, 'row', [(line[0], line[y]) for line in LINE])  7.18 us
    pallas_call x1, Pallas kernels, final_call(): pl.pallas_call(final_kernel, out_shape=jax.ShapeDtypeStruct((rows, cols),...  5.76 us
    all_gather x1, blocking collectives, per_device(): panel = lax.all_gather(panel, 'col', axis_index_groups=PAIR)[0]  1.99 us
    all_gather x1, blocking collectives, per_device(): block = lax.all_gather(strip[:, :PIVOT], 'col', axis_index_groups=PAIR)[0]  1.85 us
  transfers between devices with their start and end apart: 15, of which 6 were waited for; matrix products, arithmetic and copies ran while one was open for 0% of the time, Pallas kernels for 18%

profile of v3, /device:TPU:0, one launch (start us, length us, event | category | flops | bytes accessed | tf_op | source)
XLA Modules:
  0.0 57.5 jit_solution(15179744553276891253)
XLA Ops:
  0.0 0.0 slice-start
  0.0 1.1 %slice.51 = s32[128,1024]{1,0:T(8,128)S(1)} slice(s32[512,1024]{1,0:T(8,128)} %refs_4_.1), slice={[0:128], [0:1024]} | slice | bytes 1048576 | tf_op jit(solution)/shard_map/slice | solution.py:241
  1.2 1.9 %all-gather = bf16[256,128]{1,0:T(8,128)(2,1)S(1)} all-gather(bf16[128,128]{1,0:T(8,128)(2,1)S(1)} %slice.71), channel_id=2, replica_groups={{0,1},{2,3},{4,5},{6,7},{8,9},{10,11},{12,13},{14,15},{16,17},{18,19},{..., dimensions={0}, use_global_device_ids=true | all-gather | bytes 98304 | tf_op jit(solution)/shard_map/all_gather | solution.py:242
  3.1 3.6 %collective-permute-start.2 = (bf16[128,384]{1,0:T(8,128)(2,1)S(1)}, bf16[128,384]{1,0:T(8,128)(2,1)S(1)}, u32[]{:S(2)}, u32[]{:S(2)}) collective-permute-start(bf16[128,384]{1,0:T(8,128)(2,1)S(1)} %get-tuple-element.9), channel_id=1, source_target_pairs={{0,8},{32,40},{64,72},{96,104},{1,9},{33,41},{65,73},{97,105},{2,1... | collective-permute-start | bytes 294920 | tf_op jit(solution)/shard_map/ppermute | solution.py:248
  6.7 2.3 %collective-permute-start.1 = (bf16[128,384]{1,0:T(8,128)(2,1)S(1)}, bf16[128,384]{1,0:T(8,128)(2,1)S(1)}, u32[]{:S(2)}, u32[]{:S(2)}) collective-permute-start(bf16[128,384]{1,0:T(8,128)(2,1)S(1)} %get-tuple-element.10), channel_id=1, source_target_pairs={{0,16},{32,48},{64,80},{96,112},{1,17},{33,49},{65,81},{97,113},{2... | collective-permute-start | bytes 294920 | tf_op jit(solution)/shard_map/ppermute | solution.py:248
  9.0 1.3 %collective-permute-start = (bf16[128,384]{1,0:T(8,128)(2,1)S(1)}, bf16[128,384]{1,0:T(8,128)(2,1)S(1)}, u32[]{:S(2)}, u32[]{:S(2)}) collective-permute-start(bf16[128,384]{1,0:T(8,128)(2,1)S(1)} %get-tuple-element.11), channel_id=1, source_target_pairs={{0,24},{32,56},{64,88},{96,120},{1,25},{33,57},{65,89},{97,121},{2... | collective-permute-start | bytes 294920 | tf_op jit(solution)/shard_map/ppermute | solution.py:248
  10.3 0.0 slice-done
  10.4 2.0 %all-gather.1 = bf16[1024,128]{1,0:T(8,128)(2,1)S(1)} all-gather(bf16[512,128]{1,0:T(8,128)(2,1)S(1)} %convert_element_type.7), channel_id=3, replica_groups={{0,1},{2,3},{4,5},{6,7},{8,9},{10,11},{12,13},{14,15},{16,17},{18,19},{..., dimensions={0}, use_global_device_ids=true | all-gather | bytes 393216 | tf_op jit(solution)/shard_map/all_gather | solution.py:244
  12.4 4.1 %collective-permute-start.11 = (bf16[512,128]{1,0:T(8,128)(2,1)S(1)}, bf16[512,128]{1,0:T(8,128)(2,1)S(1)}, u32[]{:S(2)}, u32[]{:S(2)}) collective-permute-start(bf16[512,128]{1,0:T(8,128)(2,1)S(1)} %slice.80.refs_4_), channel_id=1, source_target_pairs={{0,6},{2,0},{4,2},{6,4},{1,7},{3,1},{5,3},{7,5},{8,14},{10,8},{12,... | collective-permute-start | bytes 393224 | tf_op jit(solution)/shard_map/ppermute | solution.py:235
  16.5 0.0 collective-permute-start.10
  16.5 0.0 collective-permute-done.2
  16.5 1.3 %collective-permute-start.9 = (bf16[512,128]{1,0:T(8,128)(2,1)S(1)}, bf16[512,128]{1,0:T(8,128)(2,1)S(1)}, u32[]{:S(2)}, u32[]{:S(2)}) collective-permute-start(bf16[512,128]{1,0:T(8,128)(2,1)S(1)} %slice.80.refs_4_), channel_id=1, source_target_pairs={{0,2},{2,4},{4,6},{6,0},{1,3},{3,5},{5,7},{7,1},{8,10},{10,12},{12... | collective-permute-start | bytes 393224 | tf_op jit(solution)/shard_map/ppermute | solution.py:235
  17.7 0.0 collective-permute-done.1
  17.8 0.0 collective-permute-done
  17.8 0.1 fusion.2
  17.8 2.8 %collective-permute-start.5 = (bf16[128,384]{1,0:T(8,128)(2,1)S(1)}, bf16[128,384]{1,0:T(8,128)(2,1)S(1)}, u32[]{:S(2)}, u32[]{:S(2)}) collective-permute-start(bf16[128,384]{1,0:T(8,128)(2,1)S(1)} %fusion.2), channel_id=1, source_target_pairs={{0,96},{32,0},{64,32},{96,64},{8,104},{40,8},{72,40},{104,72},{16,... | collective-permute-start | bytes 294920 | tf_op jit(solution)/shard_map/ppermute | solution.py:235
  20.7 0.8 %collective-permute-start.4 = (bf16[128,384]{1,0:T(8,128)(2,1)S(1)}, bf16[128,384]{1,0:T(8,128)(2,1)S(1)}, u32[]{:S(2)}, u32[]{:S(2)}) collective-permute-start(bf16[128,384]{1,0:T(8,128)(2,1)S(1)} %fusion.2), channel_id=1, source_target_pairs={{0,64},{32,96},{64,0},{96,32},{8,72},{40,104},{72,8},{104,40},{16,... | collective-permute-start | bytes 294920 | tf_op jit(solution)/shard_map/ppermute | solution.py:235
  21.5 3.1 %collective-permute-done.5 = bf16[128,384]{1,0:T(8,128)(2,1)S(1)} collective-permute-done((bf16[128,384]{1,0:T(8,128)(2,1)S(1)}, bf16[128,384]{1,0:T(8,128)(2,1)S(1)}, u32[]{:S(2)}, u32[]{:S(2)}) %collective-permute-start.5) | collective-permute-done | bytes 98336 | tf_op jit(solution)/shard_map/ppermute | solution.py:235
  24.5 0.5 collective-permute-start.3
  25.1 1.8 %collective-permute-done.4 = bf16[128,384]{1,0:T(8,128)(2,1)S(1)} collective-permute-done((bf16[128,384]{1,0:T(8,128)(2,1)S(1)}, bf16[128,384]{1,0:T(8,128)(2,1)S(1)}, u32[]{:S(2)}, u32[]{:S(2)}) %collective-permute-start.4) | collective-permute-done | bytes 98336 | tf_op jit(solution)/shard_map/ppermute | solution.py:235
  26.9 3.9 %collective-permute-done.3 = bf16[128,384]{1,0:T(8,128)(2,1)S(1)} collective-permute-done((bf16[128,384]{1,0:T(8,128)(2,1)S(1)}, bf16[128,384]{1,0:T(8,128)(2,1)S(1)}, u32[]{:S(2)}, u32[]{:S(2)}) %collective-permute-start.3) | collective-permute-done | bytes 98336 | tf_op jit(solution)/shard_map/ppermute | solution.py:235
  30.8 2.2 %collective-permute-start.8 = (bf16[4,128,128]{2,1,0:T(8,128)(2,1)S(1)}, bf16[4,128,128]{2,1,0:T(8,128)(2,1)S(1)}, u32[]{:S(2)}, u32[]{:S(2)}) collective-permute-start(bf16[4,128,128]{2,1,0:T(8,128)(2,1)S(1)} %pad_maximum_fusion.5.refs_0_), channel_id=1, source_target_pairs={{0,6},{2,0},{4,2},{6,4},{1,7},{3,1},{5,3},{7,5},{8,14},{10,8},{12,... | collective-permute-start | bytes 393224 | tf_op jit(solution)/shard_map/ppermute | solution.py:235
  33.0 2.2 %collective-permute-start.7 = (bf16[4,128,128]{2,1,0:T(8,128)(2,1)S(1)}, bf16[4,128,128]{2,1,0:T(8,128)(2,1)S(1)}, u32[]{:S(2)}, u32[]{:S(2)}) collective-permute-start(bf16[4,128,128]{2,1,0:T(8,128)(2,1)S(1)} %pad_maximum_fusion.5.refs_0_), channel_id=1, source_target_pairs={{0,4},{2,6},{4,0},{6,2},{1,5},{3,7},{5,1},{7,3},{8,12},{10,14},{12... | collective-permute-start | bytes 393224 | tf_op jit(solution)/shard_map/ppermute | solution.py:235
  35.2 0.0 collective-permute-done.11.refs_7_
  35.2 0.1 collective-permute-start.6
  35.3 0.0 copy-start
  35.3 0.0 collective-permute-done.10.refs_6_
  35.4 0.1 collective-permute-start.14
  35.4 0.0 collective-permute-done.9.refs_5_
  35.4 0.1 collective-permute-start.13
  35.5 0.5 collective-permute-done.8.refs_3_
  36.0 1.7 %collective-permute-start.12 = (bf16[4,128,256]{2,1,0:T(8,128)(2,1)S(1)}, bf16[4,128,256]{2,1,0:T(8,128)(2,1)S(1)}, u32[]{:S(2)}, u32[]{:S(2)}) collective-permute-start(bf16[4,128,256]{2,1,0:T(8,128)(2,1)S(1)} %pad_maximum_fusion.refs_0_), channel_id=1, source_target_pairs={{0,8},{8,16},{16,24},{24,0},{32,40},{40,48},{48,56},{56,32},{64,72... | collective-permute-start | bytes 786440 | tf_op jit(solution)/shard_map/ppermute | solution.py:235
  37.7 1.7 %collective-permute-done.7.refs_2_ = bf16[4,128,128]{2,1,0:T(8,128)(2,1)S(1)} collective-permute-done((bf16[4,128,128]{2,1,0:T(8,128)(2,1)S(1)}, bf16[4,128,128]{2,1,0:T(8,128)(2,1)S(1)}, u32[]{:S(2)}, u32[]{:S(2)}) %collective-permute-start.7) | collective-permute-done | bytes 131104 | tf_op jit(solution)/shard_map/ppermute | solution.py:235
  39.5 2.0 %collective-permute-done.6.refs_1_ = bf16[4,128,128]{2,1,0:T(8,128)(2,1)S(1)} collective-permute-done((bf16[4,128,128]{2,1,0:T(8,128)(2,1)S(1)}, bf16[4,128,128]{2,1,0:T(8,128)(2,1)S(1)}, u32[]{:S(2)}, u32[]{:S(2)}) %collective-permute-start.6) | collective-permute-done | bytes 131104 | tf_op jit(solution)/shard_map/ppermute | solution.py:235
  41.4 10.1 %chain.1.own_ref = bf16[512,512]{1,0:T(8,128)(2,1)S(1)} custom-call(bf16[4,128,128]{2,1,0:T(8,128)(2,1)S(1)} %pad_maximum_fusion.5.refs_0_, bf16[4,128,128]{2,1,0:T(8,128)(2,1)S(1)} %collective-permute-done.6.refs_1_, bf16[4,128,128]{2,1,0:T(8,128)(2,1)S(1)} %collective-permute-done.7.refs_2_, bf16[4,128,128]{2,1,0:T(8,128)(2,1)S(1)} %collective-permute-done.8.refs_3_, ...), custom_call_target="tpu_custom_call" | custom-call | flops 14000000000 | bytes 2000000 | tf_op jit(solution)/shard_map/chain/pallas_call | solution.py:192
  51.5 0.0 collective-permute-done.14.refs_3_
  51.5 0.0 collective-permute-done.13.refs_2_
  51.5 0.0 collective-permute-done.12.refs_1_
  51.5 0.0 copy-done
  51.6 5.8 %final.1 = s32[512,1024]{1,0:T(8,128)} custom-call(bf16[512,512]{1,0:T(8,128)(2,1)S(1)} %chain.1.own_ref, bf16[4,128,256]{2,1,0:T(8,128)(2,1)S(1)} %pad_maximum_fusion.refs_0_, bf16[4,128,256]{2,1,0:T(8,128)(2,1)S(1)} %collective-permute-done.12.refs_1_, bf16[4,128,256]{2,1,0:T(8,128)(2,1)S(1)} %collective-permute-done.13.refs_2_, ...), custom_call_target="tpu_custom_call" | custom-call | flops 4000000000 | bytes 2000000 | tf_op jit(solution)/shard_map/final/pallas_call | solution.py:213
  (17 shorter events, 0.2 us)
Async XLA Ops:
  0.0 10.3 %slice-start = ((s32[512,1024]{1,0:T(8,128)}), s32[512,128]{1,0:T(8,128)S(1)}, s32[]{:S(2)}) async-start(s32[512,1024]{1,0:T(8,128)} %refs_4_.1), calls=%async_computation | async-start | bytes 524288 | tf_op jit(solution)/shard_map/slice | solution.py:243
  3.1 13.4 %collective-permute-start.2 = (bf16[128,384]{1,0:T(8,128)(2,1)S(1)}, bf16[128,384]{1,0:T(8,128)(2,1)S(1)}, u32[]{:S(2)}, u32[]{:S(2)}) collective-permute-start(bf16[128,384]{1,0:T(8,128)(2,1)S(1)} %get-tuple-element.9), channel_id=1, source_target_pairs={{0,8},{32,40},{64,72},{96,104},{1,9},{33,41},{65,73},{97,105},{2,1... | collective-permute-start | bytes 294920 | tf_op jit(solution)/shard_map/ppermute | solution.py:248
  6.7 11.0 %collective-permute-start.1 = (bf16[128,384]{1,0:T(8,128)(2,1)S(1)}, bf16[128,384]{1,0:T(8,128)(2,1)S(1)}, u32[]{:S(2)}, u32[]{:S(2)}) collective-permute-start(bf16[128,384]{1,0:T(8,128)(2,1)S(1)} %get-tuple-element.10), channel_id=1, source_target_pairs={{0,16},{32,48},{64,80},{96,112},{1,17},{33,49},{65,81},{97,113},{2... | collective-permute-start | bytes 294920 | tf_op jit(solution)/shard_map/ppermute | solution.py:248
  9.0 8.7 %collective-permute-start = (bf16[128,384]{1,0:T(8,128)(2,1)S(1)}, bf16[128,384]{1,0:T(8,128)(2,1)S(1)}, u32[]{:S(2)}, u32[]{:S(2)}) collective-permute-start(bf16[128,384]{1,0:T(8,128)(2,1)S(1)} %get-tuple-element.11), channel_id=1, source_target_pairs={{0,24},{32,56},{64,88},{96,120},{1,25},{33,57},{65,89},{97,121},{2... | collective-permute-start | bytes 294920 | tf_op jit(solution)/shard_map/ppermute | solution.py:248
  12.4 22.8 %collective-permute-start.11 = (bf16[512,128]{1,0:T(8,128)(2,1)S(1)}, bf16[512,128]{1,0:T(8,128)(2,1)S(1)}, u32[]{:S(2)}, u32[]{:S(2)}) collective-permute-start(bf16[512,128]{1,0:T(8,128)(2,1)S(1)} %slice.80.refs_4_), channel_id=1, source_target_pairs={{0,6},{2,0},{4,2},{6,4},{1,7},{3,1},{5,3},{7,5},{8,14},{10,8},{12,... | collective-permute-start | bytes 393224 | tf_op jit(solution)/shard_map/ppermute | solution.py:235
  16.5 18.9 %collective-permute-start.10 = (bf16[512,128]{1,0:T(8,128)(2,1)S(1)}, bf16[512,128]{1,0:T(8,128)(2,1)S(1)}, u32[]{:S(2)}, u32[]{:S(2)}) collective-permute-start(bf16[512,128]{1,0:T(8,128)(2,1)S(1)} %slice.80.refs_4_), channel_id=1, source_target_pairs={{0,4},{2,6},{4,0},{6,2},{1,5},{3,7},{5,1},{7,3},{8,12},{10,14},{12... | collective-permute-start | bytes 393224 | tf_op jit(solution)/shard_map/ppermute | solution.py:235
  16.5 18.9 %collective-permute-start.9 = (bf16[512,128]{1,0:T(8,128)(2,1)S(1)}, bf16[512,128]{1,0:T(8,128)(2,1)S(1)}, u32[]{:S(2)}, u32[]{:S(2)}) collective-permute-start(bf16[512,128]{1,0:T(8,128)(2,1)S(1)} %slice.80.refs_4_), channel_id=1, source_target_pairs={{0,2},{2,4},{4,6},{6,0},{1,3},{3,5},{5,7},{7,1},{8,10},{10,12},{12... | collective-permute-start | bytes 393224 | tf_op jit(solution)/shard_map/ppermute | solution.py:235
  17.8 6.7 %collective-permute-start.5 = (bf16[128,384]{1,0:T(8,128)(2,1)S(1)}, bf16[128,384]{1,0:T(8,128)(2,1)S(1)}, u32[]{:S(2)}, u32[]{:S(2)}) collective-permute-start(bf16[128,384]{1,0:T(8,128)(2,1)S(1)} %fusion.2), channel_id=1, source_target_pairs={{0,96},{32,0},{64,32},{96,64},{8,104},{40,8},{72,40},{104,72},{16,... | collective-permute-start | bytes 294920 | tf_op jit(solution)/shard_map/ppermute | solution.py:235
  20.7 6.2 %collective-permute-start.4 = (bf16[128,384]{1,0:T(8,128)(2,1)S(1)}, bf16[128,384]{1,0:T(8,128)(2,1)S(1)}, u32[]{:S(2)}, u32[]{:S(2)}) collective-permute-start(bf16[128,384]{1,0:T(8,128)(2,1)S(1)} %fusion.2), channel_id=1, source_target_pairs={{0,64},{32,96},{64,0},{96,32},{8,72},{40,104},{72,8},{104,40},{16,... | collective-permute-start | bytes 294920 | tf_op jit(solution)/shard_map/ppermute | solution.py:235
  24.5 6.3 %collective-permute-start.3 = (bf16[128,384]{1,0:T(8,128)(2,1)S(1)}, bf16[128,384]{1,0:T(8,128)(2,1)S(1)}, u32[]{:S(2)}, u32[]{:S(2)}) collective-permute-start(bf16[128,384]{1,0:T(8,128)(2,1)S(1)} %fusion.2), channel_id=1, source_target_pairs={{0,32},{32,64},{64,96},{96,0},{8,40},{40,72},{72,104},{104,8},{16,... | collective-permute-start | bytes 294920 | tf_op jit(solution)/shard_map/ppermute | solution.py:235
  30.8 5.2 %collective-permute-start.8 = (bf16[4,128,128]{2,1,0:T(8,128)(2,1)S(1)}, bf16[4,128,128]{2,1,0:T(8,128)(2,1)S(1)}, u32[]{:S(2)}, u32[]{:S(2)}) collective-permute-start(bf16[4,128,128]{2,1,0:T(8,128)(2,1)S(1)} %pad_maximum_fusion.5.refs_0_), channel_id=1, source_target_pairs={{0,6},{2,0},{4,2},{6,4},{1,7},{3,1},{5,3},{7,5},{8,14},{10,8},{12,... | collective-permute-start | bytes 393224 | tf_op jit(solution)/shard_map/ppermute | solution.py:235
  33.0 6.5 %collective-permute-start.7 = (bf16[4,128,128]{2,1,0:T(8,128)(2,1)S(1)}, bf16[4,128,128]{2,1,0:T(8,128)(2,1)S(1)}, u32[]{:S(2)}, u32[]{:S(2)}) collective-permute-start(bf16[4,128,128]{2,1,0:T(8,128)(2,1)S(1)} %pad_maximum_fusion.5.refs_0_), channel_id=1, source_target_pairs={{0,4},{2,6},{4,0},{6,2},{1,5},{3,7},{5,1},{7,3},{8,12},{10,14},{12... | collective-permute-start | bytes 393224 | tf_op jit(solution)/shard_map/ppermute | solution.py:235
  35.2 6.2 %collective-permute-start.6 = (bf16[4,128,128]{2,1,0:T(8,128)(2,1)S(1)}, bf16[4,128,128]{2,1,0:T(8,128)(2,1)S(1)}, u32[]{:S(2)}, u32[]{:S(2)}) collective-permute-start(bf16[4,128,128]{2,1,0:T(8,128)(2,1)S(1)} %pad_maximum_fusion.5.refs_0_), channel_id=1, source_target_pairs={{0,2},{2,4},{4,6},{6,0},{1,3},{3,5},{5,7},{7,1},{8,10},{10,12},{12... | collective-permute-start | bytes 393224 | tf_op jit(solution)/shard_map/ppermute | solution.py:235
  35.3 16.2 %copy-start = (s32[512,1024]{1,0:T(8,128)S(1)}, s32[512,1024]{1,0:T(8,128)}, u32[]{:S(2)}) copy-start(s32[512,1024]{1,0:T(8,128)} %refs_4_.1) | copy-start | bytes 6291460
  35.4 16.2 %collective-permute-start.14 = (bf16[4,128,256]{2,1,0:T(8,128)(2,1)S(1)}, bf16[4,128,256]{2,1,0:T(8,128)(2,1)S(1)}, u32[]{:S(2)}, u32[]{:S(2)}) collective-permute-start(bf16[4,128,256]{2,1,0:T(8,128)(2,1)S(1)} %pad_maximum_fusion.refs_0_), channel_id=1, source_target_pairs={{0,24},{8,0},{16,8},{24,16},{32,56},{40,32},{48,40},{56,48},{64,88... | collective-permute-start | bytes 786440 | tf_op jit(solution)/shard_map/ppermute | solution.py:235
  35.4 16.1 %collective-permute-start.13 = (bf16[4,128,256]{2,1,0:T(8,128)(2,1)S(1)}, bf16[4,128,256]{2,1,0:T(8,128)(2,1)S(1)}, u32[]{:S(2)}, u32[]{:S(2)}) collective-permute-start(bf16[4,128,256]{2,1,0:T(8,128)(2,1)S(1)} %pad_maximum_fusion.refs_0_), channel_id=1, source_target_pairs={{0,16},{8,24},{16,0},{24,8},{32,48},{40,56},{48,32},{56,40},{64,80... | collective-permute-start | bytes 786440 | tf_op jit(solution)/shard_map/ppermute | solution.py:235
  36.0 15.5 %collective-permute-start.12 = (bf16[4,128,256]{2,1,0:T(8,128)(2,1)S(1)}, bf16[4,128,256]{2,1,0:T(8,128)(2,1)S(1)}, u32[]{:S(2)}, u32[]{:S(2)}) collective-permute-start(bf16[4,128,256]{2,1,0:T(8,128)(2,1)S(1)} %pad_maximum_fusion.refs_0_), channel_id=1, source_target_pairs={{0,8},{8,16},{16,24},{24,0},{32,40},{40,48},{48,56},{56,32},{64,72... | collective-permute-start | bytes 786440 | tf_op jit(solution)/shard_map/ppermute | solution.py:235

commit v4 on v3

--- a/solution.py
+++ b/solution.py
@@ -81,8 +81,10 @@
 
 def square(x_ref, at, tab_ref):
     cols = slice(at, at + HALF)
-    lower(x_ref, at, cols, sums(tab_ref, tab_ref, ALL, ALL))
-    encode_rows(x_ref, at, cols, HALF, tab_ref)
+    parts = [sums(tab_ref, tab_ref, slice(r, r + PIVOT), ALL) for r in (0, PIVOT)]
+    for n, part in enumerate(parts):
+        lower(x_ref, at + n * PIVOT, cols, part)
+        encode_rows(x_ref, at + n * PIVOT, cols, PIVOT, tab_ref, n * PIVOT)
 
 
 def close(x_ref, at, tab_ref):
@@ -239,11 +241,13 @@
 def per_device(weights):
     row = lax.axis_index("row")
     strip = lax.optimization_barrier(weights[:PIVOT, :]).astype(BF16)
-    block = lax.all_gather(strip[:, :PIVOT], "col", axis_index_groups=PAIR)[0]
+    roots = [(line[0] * lax.axis_size("col") + a, line[0] * lax.axis_size("col") + b) for line in LINE for a, b in PAIR]
+    block = lax.ppermute(strip[:, :PIVOT], ("row", "col"), roots)
+    block = jnp.where(lax.axis_index("col") % 2 == 0, strip[:, :PIVOT], block)
     panel = lax.optimization_barrier(weights[:, :PIVOT]).astype(BF16)
     panel = lax.all_gather(panel, "col", axis_index_groups=PAIR)[0]
     message = jnp.concatenate([strip[:, :HALF], block], axis=1)
-    for y in range(1, SIDE):
+    for y in (3, 2, 1):
         sent = jnp.concatenate([strip[:, y * HALF : (y + 1) * HALF], block], axis=1)
         got = lax.ppermute(sent, "row", [(line[0], line[y]) for line in LINE])
         message = jnp.where(row % SIDE == y, got, message)

time: 57.7 us -> 56.4 us (0.977)
  blocking collectives: 3.85 us -> 1.99 us
  starting transfers between devices: 23 us -> 23.8 us
    all_gather x1 -> x0, blocking collectives: 1.85 us -> none  [per_device(): block = lax.all_gather(strip[:, :PIVOT], 'col', axis_index_groups=PAIR)[0]]
    ppermute x0 -> x1, starting transfers between devices: none -> 1.29 us  [per_device(): block = lax.ppermute(strip[:, :PIVOT], ('row', 'col'), roots)]
    ppermute x3, starting transfers between devices: 7.18 us -> 6.21 us  [per_device(): got = lax.ppermute(sent, 'row', [(line[0], line[y]) for line in LINE])]
    ppermute x0 -> x1, waiting for transfers between devices: none -> 0.8 us  [per_device(): block = lax.ppermute(strip[:, :PIVOT], ('row', 'col'), roots)]
  transfers between devices with their start and end apart: 15 -> 16, of which waited for: 6 -> 6; matrix products, arithmetic and copies ran while one was open for 0% -> 0% of each run, Pallas kernels for 18% -> 17%
where the time goes in v4:
time: 56.4 us; the launch traced here: 56.2 us
  starting transfers between devices  23.8 us (42%)
  Pallas kernels  15.3 us (27%)
  waiting for transfers between devices  13.3 us (24%)
  blocking collectives  1.99 us (4%)
  local copies, waits for them, and re-layouts  1.23 us (2%)
    ppermute x12, starting transfers between devices, gather_line(): got[shift] = lax.ppermute(array, axis, pairs)  16.3 us
    ppermute x12, waiting for transfers between devices, gather_line(): got[shift] = lax.ppermute(array, axis, pairs)  12.5 us
    pallas_call x1, Pallas kernels, chain_call(): pl.pallas_call(chain_kernel, out_shape=jax.ShapeDtypeStruct((rows, SIZE),...  9.52 us
    ppermute x3, starting transfers between devices, per_device(): got = lax.ppermute(sent, 'row', [(line[0], line[y]) for line in LINE])  6.21 us
    pallas_call x1, Pallas kernels, final_call(): pl.pallas_call(final_kernel, out_shape=jax.ShapeDtypeStruct((rows, cols),...  5.77 us
    all_gather x1, blocking collectives, per_device(): panel = lax.all_gather(panel, 'col', axis_index_groups=PAIR)[0]  1.99 us
    ppermute x1, starting transfers between devices, per_device(): block = lax.ppermute(strip[:, :PIVOT], ('row', 'col'), roots)  1.29 us
    slice x1, local copies, waits for them, and re-layouts, per_device(): strip = lax.optimization_barrier(weights[:PIVOT, :]).astype(BF16)  1.15 us
  transfers between devices with their start and end apart: 16, of which 6 were waited for; matrix products, arithmetic and copies ran while one was open for 0% of the time, Pallas kernels for 17%

profile of v4, /device:TPU:0, one launch (start us, length us, event | category | flops | bytes accessed | tf_op | source)
XLA Modules:
  0.0 56.2 jit_solution(7960922372800152052)
XLA Ops:
  0.0 0.0 slice-start
  0.0 1.1 %slice.49 = s32[128,1024]{1,0:T(8,128)S(1)} slice(s32[512,1024]{1,0:T(8,128)} %refs_4_.1), slice={[0:128], [0:1024]} | slice | bytes 1048576 | tf_op jit(solution)/shard_map/slice | solution.py:243
  1.2 1.3 %collective-permute-start = (bf16[128,128]{1,0:T(8,128)(2,1)S(1)}, bf16[128,128]{1,0:T(8,128)(2,1)S(1)}, u32[]{:S(2)}, u32[]{:S(2)}) collective-permute-start(bf16[128,128]{1,0:T(8,128)(2,1)S(1)} %slice.67), channel_id=1, source_target_pairs={{0,1},{2,3},{4,5},{6,7},{32,33},{34,35},{36,37},{38,39},{64,65},{6... | collective-permute-start | bytes 98312 | tf_op jit(solution)/shard_map/ppermute | solution.py:245
  2.6 0.8 %collective-permute-done = bf16[128,128]{1,0:T(8,128)(2,1)S(1)} collective-permute-done((bf16[128,128]{1,0:T(8,128)(2,1)S(1)}, bf16[128,128]{1,0:T(8,128)(2,1)S(1)}, u32[]{:S(2)}, u32[]{:S(2)}) %collective-permute-start) | collective-permute-done | bytes 32800 | tf_op jit(solution)/shard_map/ppermute | solution.py:245
  3.4 3.6 %collective-permute-start.3 = (bf16[128,384]{1,0:T(8,128)(2,1)S(1)}, bf16[128,384]{1,0:T(8,128)(2,1)S(1)}, u32[]{:S(2)}, u32[]{:S(2)}) collective-permute-start(bf16[128,384]{1,0:T(8,128)(2,1)S(1)} %get-tuple-element.9), channel_id=1, source_target_pairs={{0,24},{32,56},{64,88},{96,120},{1,25},{33,57},{65,89},{97,121},{2... | collective-permute-start | bytes 294920 | tf_op jit(solution)/shard_map/ppermute | solution.py:252
  7.0 1.3 %collective-permute-start.2 = (bf16[128,384]{1,0:T(8,128)(2,1)S(1)}, bf16[128,384]{1,0:T(8,128)(2,1)S(1)}, u32[]{:S(2)}, u32[]{:S(2)}) collective-permute-start(bf16[128,384]{1,0:T(8,128)(2,1)S(1)} %get-tuple-element.10), channel_id=1, source_target_pairs={{0,16},{32,48},{64,80},{96,112},{1,17},{33,49},{65,81},{97,113},{2... | collective-permute-start | bytes 294920 | tf_op jit(solution)/shard_map/ppermute | solution.py:252
  8.3 1.3 %collective-permute-start.1 = (bf16[128,384]{1,0:T(8,128)(2,1)S(1)}, bf16[128,384]{1,0:T(8,128)(2,1)S(1)}, u32[]{:S(2)}, u32[]{:S(2)}) collective-permute-start(bf16[128,384]{1,0:T(8,128)(2,1)S(1)} %get-tuple-element.11), channel_id=1, source_target_pairs={{0,8},{32,40},{64,72},{96,104},{1,9},{33,41},{65,73},{97,105},{2,1... | collective-permute-start | bytes 294920 | tf_op jit(solution)/shard_map/ppermute | solution.py:252
  9.6 0.0 slice-done
  9.7 2.0 %all-gather = bf16[1024,128]{1,0:T(8,128)(2,1)S(1)} all-gather(bf16[512,128]{1,0:T(8,128)(2,1)S(1)} %convert_element_type.7), channel_id=2, replica_groups={{0,1},{2,3},{4,5},{6,7},{8,9},{10,11},{12,13},{14,15},{16,17},{18,19},{..., dimensions={0}, use_global_device_ids=true | all-gather | bytes 393216 | tf_op jit(solution)/shard_map/all_gather | solution.py:248
  11.7 4.1 %collective-permute-start.12 = (bf16[512,128]{1,0:T(8,128)(2,1)S(1)}, bf16[512,128]{1,0:T(8,128)(2,1)S(1)}, u32[]{:S(2)}, u32[]{:S(2)}) collective-permute-start(bf16[512,128]{1,0:T(8,128)(2,1)S(1)} %slice.75.refs_4_), channel_id=1, source_target_pairs={{0,6},{2,0},{4,2},{6,4},{1,7},{3,1},{5,3},{7,5},{8,14},{10,8},{12,... | collective-permute-start | bytes 393224 | tf_op jit(solution)/shard_map/ppermute | solution.py:237
  15.8 0.0 collective-permute-start.11
  15.8 0.0 collective-permute-done.3
  15.8 1.3 %collective-permute-start.10 = (bf16[512,128]{1,0:T(8,128)(2,1)S(1)}, bf16[512,128]{1,0:T(8,128)(2,1)S(1)}, u32[]{:S(2)}, u32[]{:S(2)}) collective-permute-start(bf16[512,128]{1,0:T(8,128)(2,1)S(1)} %slice.75.refs_4_), channel_id=1, source_target_pairs={{0,2},{2,4},{4,6},{6,0},{1,3},{3,5},{5,7},{7,1},{8,10},{10,12},{12... | collective-permute-start | bytes 393224 | tf_op jit(solution)/shard_map/ppermute | solution.py:237
  17.1 0.0 collective-permute-done.2
  17.1 0.0 collective-permute-done.1
  17.1 0.1 fusion.2
  17.1 2.8 %collective-permute-start.6 = (bf16[128,384]{1,0:T(8,128)(2,1)S(1)}, bf16[128,384]{1,0:T(8,128)(2,1)S(1)}, u32[]{:S(2)}, u32[]{:S(2)}) collective-permute-start(bf16[128,384]{1,0:T(8,128)(2,1)S(1)} %fusion.2), channel_id=1, source_target_pairs={{0,96},{32,0},{64,32},{96,64},{8,104},{40,8},{72,40},{104,72},{16,... | collective-permute-start | bytes 294920 | tf_op jit(solution)/shard_map/ppermute | solution.py:237
  20.0 0.8 %collective-permute-start.5 = (bf16[128,384]{1,0:T(8,128)(2,1)S(1)}, bf16[128,384]{1,0:T(8,128)(2,1)S(1)}, u32[]{:S(2)}, u32[]{:S(2)}) collective-permute-start(bf16[128,384]{1,0:T(8,128)(2,1)S(1)} %fusion.2), channel_id=1, source_target_pairs={{0,64},{32,96},{64,0},{96,32},{8,72},{40,104},{72,8},{104,40},{16,... | collective-permute-start | bytes 294920 | tf_op jit(solution)/shard_map/ppermute | solution.py:237
  20.8 3.1 %collective-permute-done.6 = bf16[128,384]{1,0:T(8,128)(2,1)S(1)} collective-permute-done((bf16[128,384]{1,0:T(8,128)(2,1)S(1)}, bf16[128,384]{1,0:T(8,128)(2,1)S(1)}, u32[]{:S(2)}, u32[]{:S(2)}) %collective-permute-start.6) | collective-permute-done | bytes 98336 | tf_op jit(solution)/shard_map/ppermute | solution.py:237
  23.8 0.5 collective-permute-start.4
  24.4 1.8 %collective-permute-done.5 = bf16[128,384]{1,0:T(8,128)(2,1)S(1)} collective-permute-done((bf16[128,384]{1,0:T(8,128)(2,1)S(1)}, bf16[128,384]{1,0:T(8,128)(2,1)S(1)}, u32[]{:S(2)}, u32[]{:S(2)}) %collective-permute-start.5) | collective-permute-done | bytes 98336 | tf_op jit(solution)/shard_map/ppermute | solution.py:237
  26.2 3.9 %collective-permute-done.4 = bf16[128,384]{1,0:T(8,128)(2,1)S(1)} collective-permute-done((bf16[128,384]{1,0:T(8,128)(2,1)S(1)}, bf16[128,384]{1,0:T(8,128)(2,1)S(1)}, u32[]{:S(2)}, u32[]{:S(2)}) %collective-permute-start.4) | collective-permute-done | bytes 98336 | tf_op jit(solution)/shard_map/ppermute | solution.py:237
  30.1 2.2 %collective-permute-start.9 = (bf16[4,128,128]{2,1,0:T(8,128)(2,1)S(1)}, bf16[4,128,128]{2,1,0:T(8,128)(2,1)S(1)}, u32[]{:S(2)}, u32[]{:S(2)}) collective-permute-start(bf16[4,128,128]{2,1,0:T(8,128)(2,1)S(1)} %pad_maximum_fusion.5.refs_0_), channel_id=1, source_target_pairs={{0,6},{2,0},{4,2},{6,4},{1,7},{3,1},{5,3},{7,5},{8,14},{10,8},{12,... | collective-permute-start | bytes 393224 | tf_op jit(solution)/shard_map/ppermute | solution.py:237
  32.3 2.2 %collective-permute-start.8 = (bf16[4,128,128]{2,1,0:T(8,128)(2,1)S(1)}, bf16[4,128,128]{2,1,0:T(8,128)(2,1)S(1)}, u32[]{:S(2)}, u32[]{:S(2)}) collective-permute-start(bf16[4,128,128]{2,1,0:T(8,128)(2,1)S(1)} %pad_maximum_fusion.5.refs_0_), channel_id=1, source_target_pairs={{0,4},{2,6},{4,0},{6,2},{1,5},{3,7},{5,1},{7,3},{8,12},{10,14},{12... | collective-permute-start | bytes 393224 | tf_op jit(solution)/shard_map/ppermute | solution.py:237
  34.5 0.0 collective-permute-done.12.refs_7_
  34.5 0.1 collective-permute-start.7
  34.6 0.0 copy-start
  34.7 0.0 collective-permute-done.11.refs_6_
  34.7 0.1 collective-permute-start.15
  34.7 0.0 collective-permute-done.10.refs_5_
  34.8 1.0 %collective-permute-start.14 = (bf16[4,128,256]{2,1,0:T(8,128)(2,1)S(1)}, bf16[4,128,256]{2,1,0:T(8,128)(2,1)S(1)}, u32[]{:S(2)}, u32[]{:S(2)}) collective-permute-start(bf16[4,128,256]{2,1,0:T(8,128)(2,1)S(1)} %pad_maximum_fusion.refs_0_), channel_id=1, source_target_pairs={{0,16},{8,24},{16,0},{24,8},{32,48},{40,56},{48,32},{56,40},{64,80... | collective-permute-start | bytes 786440 | tf_op jit(solution)/shard_map/ppermute | solution.py:237
  35.7 0.0 collective-permute-done.9.refs_3_
  35.7 1.3 %collective-permute-start.13 = (bf16[4,128,256]{2,1,0:T(8,128)(2,1)S(1)}, bf16[4,128,256]{2,1,0:T(8,128)(2,1)S(1)}, u32[]{:S(2)}, u32[]{:S(2)}) collective-permute-start(bf16[4,128,256]{2,1,0:T(8,128)(2,1)S(1)} %pad_maximum_fusion.refs_0_), channel_id=1, source_target_pairs={{0,8},{8,16},{16,24},{24,0},{32,40},{40,48},{48,56},{56,32},{64,72... | collective-permute-start | bytes 786440 | tf_op jit(solution)/shard_map/ppermute | solution.py:237
  37.0 1.7 %collective-permute-done.8.refs_2_ = bf16[4,128,128]{2,1,0:T(8,128)(2,1)S(1)} collective-permute-done((bf16[4,128,128]{2,1,0:T(8,128)(2,1)S(1)}, bf16[4,128,128]{2,1,0:T(8,128)(2,1)S(1)}, u32[]{:S(2)}, u32[]{:S(2)}) %collective-permute-start.8) | collective-permute-done | bytes 131104 | tf_op jit(solution)/shard_map/ppermute | solution.py:237
  38.8 2.0 %collective-permute-done.7.refs_1_ = bf16[4,128,128]{2,1,0:T(8,128)(2,1)S(1)} collective-permute-done((bf16[4,128,128]{2,1,0:T(8,128)(2,1)S(1)}, bf16[4,128,128]{2,1,0:T(8,128)(2,1)S(1)}, u32[]{:S(2)}, u32[]{:S(2)}) %collective-permute-start.7) | collective-permute-done | bytes 131104 | tf_op jit(solution)/shard_map/ppermute | solution.py:237
  40.7 9.5 %chain.1.own_ref = bf16[512,512]{1,0:T(8,128)(2,1)S(1)} custom-call(bf16[4,128,128]{2,1,0:T(8,128)(2,1)S(1)} %pad_maximum_fusion.5.refs_0_, bf16[4,128,128]{2,1,0:T(8,128)(2,1)S(1)} %collective-permute-done.7.refs_1_, bf16[4,128,128]{2,1,0:T(8,128)(2,1)S(1)} %collective-permute-done.8.refs_2_, bf16[4,128,128]{2,1,0:T(8,128)(2,1)S(1)} %collective-permute-done.9.refs_3_, ...), custom_call_target="tpu_custom_call" | custom-call | flops 14000000000 | bytes 2000000 | tf_op jit(solution)/shard_map/chain/pallas_call | solution.py:194
  50.3 0.0 collective-permute-done.15.refs_3_
  50.3 0.0 collective-permute-done.14.refs_2_
  50.3 0.0 collective-permute-done.13.refs_1_
  50.3 0.0 copy-done
  50.3 5.8 %final.1 = s32[512,1024]{1,0:T(8,128)} custom-call(bf16[512,512]{1,0:T(8,128)(2,1)S(1)} %chain.1.own_ref, bf16[4,128,256]{2,1,0:T(8,128)(2,1)S(1)} %pad_maximum_fusion.refs_0_, bf16[4,128,256]{2,1,0:T(8,128)(2,1)S(1)} %collective-permute-done.13.refs_1_, bf16[4,128,256]{2,1,0:T(8,128)(2,1)S(1)} %collective-permute-done.14.refs_2_, ...), custom_call_target="tpu_custom_call" | custom-call | flops 4000000000 | bytes 2000000 | tf_op jit(solution)/shard_map/final/pallas_call | solution.py:215
  (17 shorter events, 0.2 us)
Async XLA Ops:
  0.0 9.6 %slice-start = ((s32[512,1024]{1,0:T(8,128)}), s32[512,128]{1,0:T(8,128)S(1)}, s32[]{:S(2)}) async-start(s32[512,1024]{1,0:T(8,128)} %refs_4_.1), calls=%async_computation | async-start | bytes 524288 | tf_op jit(solution)/shard_map/slice | solution.py:247
  1.2 2.1 %collective-permute-start = (bf16[128,128]{1,0:T(8,128)(2,1)S(1)}, bf16[128,128]{1,0:T(8,128)(2,1)S(1)}, u32[]{:S(2)}, u32[]{:S(2)}) collective-permute-start(bf16[128,128]{1,0:T(8,128)(2,1)S(1)} %slice.67), channel_id=1, source_target_pairs={{0,1},{2,3},{4,5},{6,7},{32,33},{34,35},{36,37},{38,39},{64,65},{6... | collective-permute-start | bytes 98312 | tf_op jit(solution)/shard_map/ppermute | solution.py:245
  3.4 12.4 %collective-permute-start.3 = (bf16[128,384]{1,0:T(8,128)(2,1)S(1)}, bf16[128,384]{1,0:T(8,128)(2,1)S(1)}, u32[]{:S(2)}, u32[]{:S(2)}) collective-permute-start(bf16[128,384]{1,0:T(8,128)(2,1)S(1)} %get-tuple-element.9), channel_id=1, source_target_pairs={{0,24},{32,56},{64,88},{96,120},{1,25},{33,57},{65,89},{97,121},{2... | collective-permute-start | bytes 294920 | tf_op jit(solution)/shard_map/ppermute | solution.py:252
  7.0 10.0 %collective-permute-start.2 = (bf16[128,384]{1,0:T(8,128)(2,1)S(1)}, bf16[128,384]{1,0:T(8,128)(2,1)S(1)}, u32[]{:S(2)}, u32[]{:S(2)}) collective-permute-start(bf16[128,384]{1,0:T(8,128)(2,1)S(1)} %get-tuple-element.10), channel_id=1, source_target_pairs={{0,16},{32,48},{64,80},{96,112},{1,17},{33,49},{65,81},{97,113},{2... | collective-permute-start | bytes 294920 | tf_op jit(solution)/shard_map/ppermute | solution.py:252
  8.3 8.7 %collective-permute-start.1 = (bf16[128,384]{1,0:T(8,128)(2,1)S(1)}, bf16[128,384]{1,0:T(8,128)(2,1)S(1)}, u32[]{:S(2)}, u32[]{:S(2)}) collective-permute-start(bf16[128,384]{1,0:T(8,128)(2,1)S(1)} %get-tuple-element.11), channel_id=1, source_target_pairs={{0,8},{32,40},{64,72},{96,104},{1,9},{33,41},{65,73},{97,105},{2,1... | collective-permute-start | bytes 294920 | tf_op jit(solution)/shard_map/ppermute | solution.py:252
  11.7 22.8 %collective-permute-start.12 = (bf16[512,128]{1,0:T(8,128)(2,1)S(1)}, bf16[512,128]{1,0:T(8,128)(2,1)S(1)}, u32[]{:S(2)}, u32[]{:S(2)}) collective-permute-start(bf16[512,128]{1,0:T(8,128)(2,1)S(1)} %slice.75.refs_4_), channel_id=1, source_target_pairs={{0,6},{2,0},{4,2},{6,4},{1,7},{3,1},{5,3},{7,5},{8,14},{10,8},{12,... | collective-permute-start | bytes 393224 | tf_op jit(solution)/shard_map/ppermute | solution.py:237
  15.8 18.9 %collective-permute-start.11 = (bf16[512,128]{1,0:T(8,128)(2,1)S(1)}, bf16[512,128]{1,0:T(8,128)(2,1)S(1)}, u32[]{:S(2)}, u32[]{:S(2)}) collective-permute-start(bf16[512,128]{1,0:T(8,128)(2,1)S(1)} %slice.75.refs_4_), channel_id=1, source_target_pairs={{0,4},{2,6},{4,0},{6,2},{1,5},{3,7},{5,1},{7,3},{8,12},{10,14},{12... | collective-permute-start | bytes 393224 | tf_op jit(solution)/shard_map/ppermute | solution.py:237
  15.8 18.9 %collective-permute-start.10 = (bf16[512,128]{1,0:T(8,128)(2,1)S(1)}, bf16[512,128]{1,0:T(8,128)(2,1)S(1)}, u32[]{:S(2)}, u32[]{:S(2)}) collective-permute-start(bf16[512,128]{1,0:T(8,128)(2,1)S(1)} %slice.75.refs_4_), channel_id=1, source_target_pairs={{0,2},{2,4},{4,6},{6,0},{1,3},{3,5},{5,7},{7,1},{8,10},{10,12},{12... | collective-permute-start | bytes 393224 | tf_op jit(solution)/shard_map/ppermute | solution.py:237
  17.1 6.7 %collective-permute-start.6 = (bf16[128,384]{1,0:T(8,128)(2,1)S(1)}, bf16[128,384]{1,0:T(8,128)(2,1)S(1)}, u32[]{:S(2)}, u32[]{:S(2)}) collective-permute-start(bf16[128,384]{1,0:T(8,128)(2,1)S(1)} %fusion.2), channel_id=1, source_target_pairs={{0,96},{32,0},{64,32},{96,64},{8,104},{40,8},{72,40},{104,72},{16,... | collective-permute-start | bytes 294920 | tf_op jit(solution)/shard_map/ppermute | solution.py:237
  20.0 6.2 %collective-permute-start.5 = (bf16[128,384]{1,0:T(8,128)(2,1)S(1)}, bf16[128,384]{1,0:T(8,128)(2,1)S(1)}, u32[]{:S(2)}, u32[]{:S(2)}) collective-permute-start(bf16[128,384]{1,0:T(8,128)(2,1)S(1)} %fusion.2), channel_id=1, source_target_pairs={{0,64},{32,96},{64,0},{96,32},{8,72},{40,104},{72,8},{104,40},{16,... | collective-permute-start | bytes 294920 | tf_op jit(solution)/shard_map/ppermute | solution.py:237
  23.8 6.3 %collective-permute-start.4 = (bf16[128,384]{1,0:T(8,128)(2,1)S(1)}, bf16[128,384]{1,0:T(8,128)(2,1)S(1)}, u32[]{:S(2)}, u32[]{:S(2)}) collective-permute-start(bf16[128,384]{1,0:T(8,128)(2,1)S(1)} %fusion.2), channel_id=1, source_target_pairs={{0,32},{32,64},{64,96},{96,0},{8,40},{40,72},{72,104},{104,8},{16,... | collective-permute-start | bytes 294920 | tf_op jit(solution)/shard_map/ppermute | solution.py:237
  30.1 5.6 %collective-permute-start.9 = (bf16[4,128,128]{2,1,0:T(8,128)(2,1)S(1)}, bf16[4,128,128]{2,1,0:T(8,128)(2,1)S(1)}, u32[]{:S(2)}, u32[]{:S(2)}) collective-permute-start(bf16[4,128,128]{2,1,0:T(8,128)(2,1)S(1)} %pad_maximum_fusion.5.refs_0_), channel_id=1, source_target_pairs={{0,6},{2,0},{4,2},{6,4},{1,7},{3,1},{5,3},{7,5},{8,14},{10,8},{12,... | collective-permute-start | bytes 393224 | tf_op jit(solution)/shard_map/ppermute | solution.py:237
  32.3 6.5 %collective-permute-start.8 = (bf16[4,128,128]{2,1,0:T(8,128)(2,1)S(1)}, bf16[4,128,128]{2,1,0:T(8,128)(2,1)S(1)}, u32[]{:S(2)}, u32[]{:S(2)}) collective-permute-start(bf16[4,128,128]{2,1,0:T(8,128)(2,1)S(1)} %pad_maximum_fusion.5.refs_0_), channel_id=1, source_target_pairs={{0,4},{2,6},{4,0},{6,2},{1,5},{3,7},{5,1},{7,3},{8,12},{10,14},{12... | collective-permute-start | bytes 393224 | tf_op jit(solution)/shard_map/ppermute | solution.py:237
  34.5 6.2 %collective-permute-start.7 = (bf16[4,128,128]{2,1,0:T(8,128)(2,1)S(1)}, bf16[4,128,128]{2,1,0:T(8,128)(2,1)S(1)}, u32[]{:S(2)}, u32[]{:S(2)}) collective-permute-start(bf16[4,128,128]{2,1,0:T(8,128)(2,1)S(1)} %pad_maximum_fusion.5.refs_0_), channel_id=1, source_target_pairs={{0,2},{2,4},{4,6},{6,0},{1,3},{3,5},{5,7},{7,1},{8,10},{10,12},{12... | collective-permute-start | bytes 393224 | tf_op jit(solution)/shard_map/ppermute | solution.py:237
  34.6 15.7 %copy-start = (s32[512,1024]{1,0:T(8,128)S(1)}, s32[512,1024]{1,0:T(8,128)}, u32[]{:S(2)}) copy-start(s32[512,1024]{1,0:T(8,128)} %refs_4_.1) | copy-start | bytes 6291460
  34.7 15.6 %collective-permute-start.15 = (bf16[4,128,256]{2,1,0:T(8,128)(2,1)S(1)}, bf16[4,128,256]{2,1,0:T(8,128)(2,1)S(1)}, u32[]{:S(2)}, u32[]{:S(2)}) collective-permute-start(bf16[4,128,256]{2,1,0:T(8,128)(2,1)S(1)} %pad_maximum_fusion.refs_0_), channel_id=1, source_target_pairs={{0,24},{8,0},{16,8},{24,16},{32,56},{40,32},{48,40},{56,48},{64,88... | collective-permute-start | bytes 786440 | tf_op jit(solution)/shard_map/ppermute | solution.py:237
  34.8 15.5 %collective-permute-start.14 = (bf16[4,128,256]{2,1,0:T(8,128)(2,1)S(1)}, bf16[4,128,256]{2,1,0:T(8,128)(2,1)S(1)}, u32[]{:S(2)}, u32[]{:S(2)}) collective-permute-start(bf16[4,128,256]{2,1,0:T(8,128)(2,1)S(1)} %pad_maximum_fusion.refs_0_), channel_id=1, source_target_pairs={{0,16},{8,24},{16,0},{24,8},{32,48},{40,56},{48,32},{56,40},{64,80... | collective-permute-start | bytes 786440 | tf_op jit(solution)/shard_map/ppermute | solution.py:237
  35.7 14.6 %collective-permute-start.13 = (bf16[4,128,256]{2,1,0:T(8,128)(2,1)S(1)}, bf16[4,128,256]{2,1,0:T(8,128)(2,1)S(1)}, u32[]{:S(2)}, u32[]{:S(2)}) collective-permute-start(bf16[4,128,256]{2,1,0:T(8,128)(2,1)S(1)} %pad_maximum_fusion.refs_0_), channel_id=1, source_target_pairs={{0,8},{8,16},{16,24},{24,0},{32,40},{40,48},{48,56},{56,32},{64,72... | collective-permute-start | bytes 786440 | tf_op jit(solution)/shard_map/ppermute | solution.py:237
